TPU v7x, 256 devices: a whole 4x4x8 slice. The times are simulated.
256 devices in a mesh: dp: 8 (over z_lo, core), cent: 32 (over y, z_hi, x).
Axes of the slice: x: 4, y: 4, z: 8 (z_hi: 2, z_lo: 4; z = z_hi * 4 + z_lo), core: 2. Of those that a mesh axis runs over, the one named last changes fastest.
Arguments:
- embeddings: bfloat16 [32768, 768], P(('dp', 'cent')), may hold values from -20 to 20
- fine_centroids: float32 [16384, 768], P('cent'), may hold values from -8 to 8
- parents: int32 [16384], P('cent'), may hold values from 0 to 2047
- coarse_centroids: float32 [2048, 768], P('cent'), may hold values from -6 to 6
Outputs:
- new_fine: float32 [16384, 768], P('cent')
- new_coarse: float32 [2048, 768], P('cent')
All inputs are finite; a program needn't handle non-finite values.
Results may differ from a plain program's by a relative error of at most 0.004.
Values may be sent and summed in bfloat16 or wider, within the bound.
No kernel may reach another device: no remote copies, remote signals or barrier semaphores. Data moves between devices by JAX's collectives and lax.ppermute only.
A program may use at most 64 MiB of HBM per device.

v0:
```python
import math

import jax
import jax.numpy as jnp
from jax import lax
from jax.sharding import PartitionSpec as P

KC = 2048


sharpness = 0.1
coarse_prior = 16.0


def copy_for_each(array, axis):
    devices = lax.axis_size(axis)
    return lax.all_to_all(
        jnp.broadcast_to(array[None], (devices, *array.shape)), axis, 0, 0, tiled=True
    )


def collected_together(array, axis):
    leaves = jax.tree.leaves(array)
    turns = sorted(range(len(leaves)), key=lambda k: -leaves[k].size)
    width = (1, *leaves[turns[0]].shape)[-1]
    lines = [
        jnp.pad(leaves[k].reshape(-1), (0, -leaves[k].size % width)).reshape(-1, width)
        for k in turns
    ]
    both, at, found = (copy_for_each(jnp.concatenate(lines), axis), 0, {})
    for k, line in zip(turns, lines):
        piece = both[:, at : at + len(line)].reshape(len(both), -1)
        found[k] = piece[:, : leaves[k].size].reshape(-1, *leaves[k].shape)
        at += len(line)
    numbers = iter(range(len(leaves)))
    return jax.tree.map(lambda _: found[next(numbers)], array)


def joined_by_halves(pieces, combine):
    while len(jax.tree.leaves(pieces)[0]) > 1:
        pieces = jax.vmap(combine)(
            *(jax.tree.map(lambda part: part[side::2], pieces) for side in (0, 1))
        )
    return jax.tree.map(lambda part: part[0], pieces)


def joined_all(array, axis, combine):
    pieces = collected_together(array, axis)
    return joined_by_halves(pieces, combine)


def cut_along(array, dim, devices):
    dims = array.shape
    tiles = array.reshape(*dims[:dim], devices, dims[dim] // devices, *dims[dim + 1 :])
    return jnp.moveaxis(tiles, dim, 0)


def summed_on_arrival(array, axis, dim):
    tiles = cut_along(array, dim, lax.axis_size(axis))
    arrived = lax.all_to_all(tiles, axis, split_axis=0, concat_axis=0, tiled=True)
    return arrived.sum(axis=0)


def side_by_side(arrays, axis, dim, along):
    widths = [math.prod(a.shape[along:]) for a in arrays]
    both = jnp.concatenate(
        [a.reshape(*a.shape[:along], w) for a, w in zip(arrays, widths)], axis=along
    )
    whole = summed_on_arrival(both, axis, dim)
    tiles = jnp.split(whole, [sum(widths[:k]) for k in range(1, len(widths))], axis=along)
    return tuple((b.reshape(*whole.shape[:along], *a.shape[along:]) for a, b in zip(arrays, tiles)))


def in_order(tiles, dim):
    dims = list(tiles.shape[1:])
    dims[dim] *= tiles.shape[0]
    return jnp.moveaxis(tiles, 0, dim).reshape(dims)


def gather_directly(array, axis, dim):
    tiles = copy_for_each(array, axis)
    return in_order(tiles, dim)


def block_logits(one_block, narrow_centroids, half_norm):
    scores = lax.dot_general(
        one_block, narrow_centroids, (((1,), (1,)), ((), ())), preferred_element_type=jnp.float32
    )
    return sharpness * (scores - half_norm[None, :])


def merge_stats(former, latter):
    highest = jnp.maximum(former[0], latter[0])
    combined = former[1] * jnp.exp(former[0] - highest) + latter[1] * jnp.exp(latter[0] - highest)
    return (highest, combined)


def coarse_terms(parent_ids, pooled, mass_rows):
    summed = jax.ops.segment_sum(pooled, parent_ids, num_segments=KC)
    weighted = jax.ops.segment_sum(mass_rows, parent_ids, num_segments=KC)
    return (summed, weighted)


def local(embeddings, fine_centroids, parents, coarse_centroids):
    gathered = lax.all_gather(embeddings, "cent", axis=0, tiled=True)
    row_count = gathered.shape[0]
    feat_width = gathered.shape[1]
    block_rows = math.gcd(row_count, 512)
    row_blocks = gathered.reshape(row_count // block_rows, block_rows, feat_width)
    narrow_centroids = fine_centroids.astype(jnp.bfloat16)
    half_norm = 0.5 * jnp.sum(fine_centroids * fine_centroids, axis=1)
    no_carry = jnp.zeros((), jnp.float32)

    def stats_step(carried, one_block):
        logits = block_logits(one_block, narrow_centroids, half_norm)
        highest = jnp.max(logits, axis=1)
        return (carried, (highest, jnp.sum(jnp.exp(logits - highest[:, None]), axis=1)))

    _, (local_peak, local_mass) = lax.scan(stats_step, no_carry, row_blocks)
    row_peak, row_mass = joined_all(
        (local_peak.reshape(-1), local_mass.reshape(-1)), "cent", merge_stats
    )

    def sum_step(carried, items):
        one_block, block_peak, block_mass = items
        logits = block_logits(one_block, narrow_centroids, half_norm)
        soft_weights = jnp.exp(logits - block_peak[:, None]) / block_mass[:, None]
        wide_block = one_block.astype(jnp.float32)
        summed = carried[0] + lax.dot_general(
            soft_weights,
            wide_block,
            (((0,), (0,)), ((), ())),
            precision=lax.Precision.HIGHEST,
            preferred_element_type=jnp.float32,
        )
        counted = carried[1] + jnp.sum(soft_weights, axis=0)
        return ((summed, counted), None)

    local_rows = fine_centroids.shape[0]
    start_state = (
        jnp.zeros(fine_centroids.shape, jnp.float32),
        jnp.zeros((local_rows,), jnp.float32),
    )
    stacked = (row_blocks, row_peak.reshape(-1, block_rows), row_mass.reshape(-1, block_rows))
    (fine_sums, fine_counts), _ = lax.scan(sum_step, start_state, stacked)
    total_sums, total_counts = lax.psum((fine_sums, fine_counts), "dp")
    pooled = fine_centroids + total_sums
    mass_rows = 1.0 + total_counts
    new_fine = pooled / mass_rows[:, None]
    col_width = feat_width // lax.axis_size("dp")
    first_col = lax.axis_index("dp") * col_width
    pooled_cols = lax.dynamic_slice_in_dim(pooled, first_col, col_width, 1)
    coarse_sum, coarse_mass = coarse_terms(parents, pooled_cols, mass_rows)
    owned_sum, owned_mass = side_by_side((coarse_sum, coarse_mass), "cent", 0, 1)
    old_cols = lax.dynamic_slice_in_dim(coarse_centroids, first_col, col_width, 1)
    new_cols = (coarse_prior * old_cols + owned_sum) / (coarse_prior + owned_mass)[:, None]
    new_coarse = gather_directly(new_cols, "dp", 1)
    return (new_fine, new_coarse)


def solution(mesh):
    in_specs = (P(("dp", "cent"), None), P("cent", None), P("cent"), P("cent", None))
    out_specs = (P("cent", None), P("cent", None))
    return jax.shard_map(local, mesh=mesh, in_specs=in_specs, out_specs=out_specs, check_vma=False)
```

profile of v0, /device:TPU:1, one launch (start us, length us, event | category | flops | bytes accessed | tf_op | source)
XLA Modules:
  0.0 385.6 jit_solution(6488801156989215922)
XLA Ops:
  7.2 0.7 all-gather.2.cloned.1.call-update
  7.9 2.2 multiply_reduce_fusion
  10.1 135.7 %all-gather.2.cloned.1.call-done = bf16[4096,768]{1,0:T(8,128)(2,1)} async-done(((bf16[128,768]{1,0:T(8,128)(2,1)}), bf16[4096,768]{1,0:T(8,128)(2,1)}) %all-gather.2.cloned.1.call-update) | async-done | bytes 6291472 | tf_op jit(solution)/shard_map/all_gather | solution.py:105
  145.9 16.8 %while.25 = (s32[]{:T(128)}, f32[8,512]{1,0:T(8,128)S(1)}, f32[8,512]{1,0:T(8,128)S(1)}, bf16[8,512,768]{2,1,0:T(8,128)(2,1)}, bf16[512,768]{1,0:T(8,128)(2,1)S(1)}, /*index=5*/f32[512]{0:T(512)S(1)}, s32[]{:T(128)}, s32[]{:T(128)}) while((s32[]{:T(128)}, f32[8,512]{1,0:T(8,128)S(1)}, f32[8,512]{1,0:T(8,128)S(1)}, ...), condition=%wide.region_4.5_spmd, body=%wide.region_1.4_spmd.sunk | while | flops 403962880 | bytes 3686505 | solution.py:119
  145.9 1.7 fusion.36
  147.6 0.2 exponential_reduce_fusion.2
  147.9 1.8 fusion.36
  149.7 0.2 exponential_reduce_fusion.2
  150.0 1.8 fusion.36
  151.8 0.2 exponential_reduce_fusion.2
  152.1 1.8 fusion.36
  153.9 0.2 exponential_reduce_fusion.2
  154.2 1.8 fusion.36
  156.0 0.2 exponential_reduce_fusion.2
  156.3 1.8 fusion.36
  158.1 0.2 exponential_reduce_fusion.2
  158.4 1.8 fusion.36
  160.2 0.2 exponential_reduce_fusion.2
  160.5 1.8 fusion.36
  162.3 0.2 exponential_reduce_fusion.2
  162.7 1.4 broadcast_in_dim.44
  164.2 5.3 %all-to-all-start = ((f32[32,2,4096]{2,1,0:T(2,128)}), f32[32,2,4096]{2,1,0:T(2,128)S(1)}, u32[]{:S(2)}, u32[]{:S(2)}) async-start(f32[32,2,4096]{2,1,0:T(2,128)} %broadcast_in_dim.44), calls=%async_computation | async-start | bytes 2097152 | tf_op jit(solution)/shard_map/all_to_all | solution.py:17
  169.5 18.9 %all-to-all-done = f32[32,2,4096]{2,1,0:T(2,128)S(1)} async-done(((f32[32,2,4096]{2,1,0:T(2,128)}), f32[32,2,4096]{2,1,0:T(2,128)S(1)}, u32[]{:S(2)}, u32[]{:S(2)}) %all-to-all-start) | async-done | bytes 1048608 | tf_op jit(solution)/shard_map/all_to_all | solution.py:17
  188.4 1.2 fusion.25
  189.6 0.6 copy_bitcast_fusion
  190.2 0.1 slice.72
  190.3 0.1 slice.71
  190.5 0.1 slice.83
  190.7 0.1 slice.82
  191.9 0.1 slice.89
  192.1 0.1 slice.88
  192.2 0.1 slice.78
  192.5 0.1 fusion.20
  192.7 40.9 %while.26 = (s32[]{:T(128)}, f32[512,768]{1,0:T(8,128)S(1)}, f32[512]{0:T(512)S(1)}, bf16[8,512,768]{2,1,0:T(8,128)(2,1)}, bf16[512,768]{1,0:T(8,128)(2,1)S(1)},...) while((s32[]{:T(128)}, f32[512,768]{1,0:T(8,128)S(1)}, ...), condition=%wide.region_7.8_spmd.clone, body=%wide.region_5.7_spmd.clone.sunk | while | flops 2820669952 | bytes 7624836 | solution.py:145
  192.7 1.9 fusion.40
  194.6 3.2 select_add_fusion.4
  197.8 1.9 fusion.40
  199.7 3.2 select_add_fusion.4
  202.9 1.9 fusion.40
  204.8 3.2 select_add_fusion.4
  208.0 1.9 fusion.40
  209.9 3.2 select_add_fusion.4
  213.2 1.9 fusion.40
  215.0 3.2 select_add_fusion.4
  218.3 1.9 fusion.40
  220.2 3.2 select_add_fusion.4
  223.4 1.9 fusion.40
  225.3 3.2 select_add_fusion.4
  228.5 1.9 fusion.40
  230.4 3.2 select_add_fusion.4
  233.6 1.1 copy-done
  234.8 22.7 %psum.15 = f32[512]{0:T(512)S(1)} all-reduce(f32[512]{0:T(512)S(1)} %get-tuple-element.81), channel_id=1, replica_groups=mesh['dp'=8,'cent'=32] {'dp'}, use_global_device_ids=true, to_apply=%region_9.10 | all-reduce | flops 512 | bytes 4096 | tf_op jit(solution)/shard_map/psum | solution.py:146
  257.5 3.4 scatter_custom_fusion.1
  260.9 0.9 concatenate.15
  261.8 56.4 %all-reduce.2.cloned.1.call-done = f32[512,768]{1,0:T(8,128)} async-done(((f32[512,768]{1,0:T(8,128)}), f32[512,768]{1,0:T(8,128)}) %all-reduce.2.cloned.1.call-update) | async-done | bytes 1572880 | tf_op jit(solution)/shard_map/psum | solution.py:146
  318.1 3.3 broadcast_divide_fusion
  321.4 3.1 scatter_custom_fusion
  324.5 0.3 pad_maximum_fusion
  324.9 36.6 %all_to_all.15 = f32[32,64,97]{2,1,0:T(8,128)S(1)} all-to-all(f32[32,64,97]{2,1,0:T(8,128)S(1)} %pad_maximum_fusion), channel_id=1, replica_groups=mesh['dp'=8,'cent'=32] {'cent'}, dimensions={0} | all-to-all | bytes 1589248 | tf_op jit(solution)/shard_map/all_to_all | solution.py:60
  361.6 0.2 fusion.17
  361.8 0.9 fusion.18
  362.8 15.0 %all_to_all.16 = f32[8,64,96]{2,1,0:T(8,128)S(1)} all-to-all(f32[8,64,96]{2,1,0:T(8,128)S(1)} %broadcast_in_dim.48), channel_id=1, replica_groups=mesh['dp'=8,'cent'=32] {'dp'}, dimensions={0} | all-to-all | bytes 393216 | tf_op jit(solution)/shard_map/all_to_all | solution.py:17
  377.8 0.2 copy.11
  378.0 0.8 reshape.47
  (68 shorter events, 2.6 us)
Async XLA Ops:
  7.2 138.7 %all-gather.2.cloned.1.call-start = ((), (), s32[]{:S(2)}) async-start(), calls=%async_computation.3 | async-start | bytes 6488064 | tf_op jit(solution)/shard_map/all_gather | solution.py:105
  162.6 1.5 copy-start.2
  164.2 24.2 %all-to-all-start = ((f32[32,2,4096]{2,1,0:T(2,128)}), f32[32,2,4096]{2,1,0:T(2,128)S(1)}, u32[]{:S(2)}, u32[]{:S(2)}) async-start(f32[32,2,4096]{2,1,0:T(2,128)} %broadcast_in_dim.44), calls=%async_computation | async-start | bytes 2097152 | tf_op jit(solution)/shard_map/all_to_all | solution.py:17
  169.4 148.7 %all-reduce.2.cloned.1.call-start = ((), (), s32[]{:S(2)}) async-start(), calls=%async_computation.4 | async-start | bytes 3145728 | tf_op jit(solution)/shard_map/psum | solution.py:146
  191.0 1.6 copy-start.3
  233.6 1.1 copy-start
  233.6 84.5 %copy-start.1 = (f32[512,768]{1,0:T(8,128)S(1)}, f32[512,768]{1,0:T(8,128)}, u32[]{:S(2)}) copy-start(f32[512,768]{1,0:T(8,128)} %param.9) | copy-start | bytes 4718596
Sparse Core Ops, SparseCore 0:
  11.4 134.4 all-gather.1
  234.9 83.1 all-reduce.1
where the time goes:
time: 387 us; the launch traced here: 386 us
  waiting for transfers between devices  212 us (55%)
  blocking collectives  74.4 us (19%)
  matrix products  54.4 us (14%)
  other arithmetic  15.7 us (4%)
  between operations  14.4 us (4%)
  local copies, waits for them, and re-layouts  9.1 us (2%)
  starting transfers between devices  5.35 us (1%)
    all_gather x1, waiting for transfers between devices, local(): gathered = lax.all_gather(embeddings, 'cent', axis=0, tiled=True)  136 us
    psum x1, waiting for transfers between devices, local(): total_sums, total_counts = lax.psum((fine_sums, fine_counts), 'dp')  56.4 us
    all_to_all x1, blocking collectives, summed_on_arrival(): lax.all_to_all(tiles, axis, split_axis=0, concat_axis=0, tiled=True)  36.6 us
    dot_general x16, matrix products, block_logits(): lax.dot_general(one_block, narrow_centroids, (((1,), (1,)), ((), ())), pr...  29 us
    dot_general x8, matrix products, sum_step(): lax.dot_general(soft_weights, wide_block, (((0,), (0,)), ((), ())), preci...  25.5 us
    psum x1, blocking collectives, local(): total_sums, total_counts = lax.psum((fine_sums, fine_counts), 'dp')  22.7 us
    all_to_all x1, waiting for transfers between devices, copy_for_each(): lax.all_to_all(jnp.broadcast_to(array[None], (devices, *array.shape)), ax...  18.9 us
    all_to_all x1, blocking collectives, copy_for_each(): lax.all_to_all(jnp.broadcast_to(array[None], (devices, *array.shape)), ax...  15 us
  transfers between devices with their start and end apart: 3, of which 3 were waited for; matrix products, arithmetic and copies ran while one was open for 2% of the time, Pallas kernels for 0%

commit v1 on v0

v1 whole, which is shorter than its diff:
```python
import jax
import jax.numpy as jnp
from jax import lax
from jax.experimental import pallas as pl
from jax.experimental.pallas import tpu as pltpu
from jax.sharding import Mesh
from jax.sharding import PartitionSpec as P


KC = 2048
D = 768
PRIOR = 16.0
LOG2E = 1.4426950408889634
SCALE = 0.1 * LOG2E
SENT_SCALE = 1.0 / 16.0
WEIGH_MB = 24
SUMS_MB = 28
bf16, f16, f32 = jnp.bfloat16, jnp.float16, jnp.float32


AXES = {"zl": 4, "core": 2, "y": 4, "zh": 2, "x": 4}


def from_ahead(array, axis, step):
    size = AXES[axis]
    if axis not in ("x", "y"):
        return lax.ppermute(array, axis, [((me + step) % size, me) for me in range(size)])
    pairs = []
    for core in (0, 1):
        for me in range(size):
            source = (me + (step if core == 0 else -step)) % size
            pairs.append((core * size + source, core * size + me))
    return lax.ppermute(array, ("core", axis), pairs)


def ring_of_four(array, axis):
    return [array] + [from_ahead(array, axis, s) for s in (1, 2, 3)]


VMEM = pl.BlockSpec(memory_space=pltpu.VMEM)


def weigh_kernel(first, n, *refs):
    skip = 2 if first else 1
    x_refs, c_refs, norm_ref = refs[skip : skip + n], refs[skip + n : skip + n + 3], refs[skip + n + 3]
    p_ref, stat_ref, x_all, norms = refs[skip + n + 4 :]
    if first:
        stat_ref[...] = refs[1][...]
    norms[512:1024, :] = jnp.broadcast_to(norm_ref[...], (128, 512)).T
    for at, c_ref in ((0, c_refs[0]), (256, c_refs[1])):
        row = c_ref[256:264, :].astype(f32)[0:1]
        row = row[:, 0:256] + row[:, 256:512] + row[:, 512:768]
        norms[at : at + 256, :] = jnp.broadcast_to(row, (128, 256)).T

    spans = ((0, 256), (256, 256), (512, 512))
    for i in range(n):
        x = x_refs[i][...]
        x_all[256 * i : 256 * i + 256, :] = x
        tops = []
        for (at, size), c_ref in zip(spans, c_refs):
            t = lax.dot_general(
                c_ref[0:size, :], x, (((1,), (1,)), ((), ())), preferred_element_type=f32
            )
            norm = norms[at : at + size, :]
            t = (t - jnp.concatenate([norm, norm], axis=1)) * SCALE
            p_ref[i, at : at + size, :] = t
            tops.append(jnp.max(t, axis=0, keepdims=True))
        top = jnp.maximum(jnp.maximum(tops[0], tops[1]), tops[2])
        mass = jnp.zeros((1, 256), f32)
        for at, size in spans:
            p = jnp.exp2(p_ref[i, at : at + size, :] - top)
            p_ref[i, at : at + size, :] = p
            mass = mass + jnp.sum(p, axis=0, keepdims=True)
        stat_ref[0, first + i : first + i + 1, :] = top
        stat_ref[1, first + i : first + i + 1, :] = mass


def weigh(place, first, stats, xs, cs, norm):
    n = len(xs)
    rows = 256 * n
    return pl.pallas_call(
        lambda *refs: weigh_kernel(first, n, *refs),
        in_specs=[pl.BlockSpec(memory_space=pltpu.SMEM)] + [VMEM] * (len(stats) + n + 4),
        out_specs=(VMEM,) * 3,
        out_shape=(
            jax.ShapeDtypeStruct((n, 1024, 256), f32),
            jax.ShapeDtypeStruct((2, 8, 256), f32),
            jax.ShapeDtypeStruct((rows, D), bf16),
        ),
        scratch_shapes=[pltpu.VMEM((1024, 128), f32)],
        cost_estimate=pl.CostEstimate(
            flops=2 * rows * 1024 * D,
            transcendentals=rows * 1024,
            bytes_accessed=2 * rows * D + 2 * 1024 * D + 4 * rows * 1024,
        ),
        compiler_params=pltpu.CompilerParams(vmem_limit_bytes=WEIGH_MB * 1024 * 1024),
    )(place, *stats, *xs, *cs, norm)


PIECES = ((0, 1, 6, 2), (3, 4, 7, 5))


def merge_kernel(rolled, last, *refs):
    parts, out_ref = refs[:4], refs[4]
    for half, pieces in enumerate(PIECES):
        for at, piece in enumerate(pieces):
            tops, masses = [], []
            for s, part in enumerate(parts):
                row = piece if half == rolled else pieces[(at - s) % 4]
                top, mass = part[0, row : row + 1, :], part[1, row : row + 1, :]
                if half == rolled and s:
                    cut = 256 - 64 * s
                    top = jnp.concatenate([top[:, cut:], top[:, :cut]], axis=1)
                    mass = jnp.concatenate([mass[:, cut:], mass[:, :cut]], axis=1)
                tops.append(top)
                masses.append(mass)
            high = jnp.maximum(jnp.maximum(tops[0], tops[1]), jnp.maximum(tops[2], tops[3]))
            total = sum(m * jnp.exp2(t - high) for m, t in zip(masses, tops))
            if last:
                own = refs[5][0, piece : piece + 1, :]
                out_ref[piece : piece + 1, :] = jnp.exp2(own - high) / total
            else:
                out_ref[0, piece : piece + 1, :] = high
                out_ref[1, piece : piece + 1, :] = total


def merge_last_kernel(rolled, *refs):
    merge_kernel(rolled, True, *refs[:4], refs[5], refs[4])


def merged_over(stat, axis, rolled, own=None):
    parts = [stat] + [from_ahead(stat, axis, s) for s in (1, 2, 3)]
    if own is None:
        kernel, shape = (lambda *refs: merge_kernel(rolled, False, *refs)), (2, 8, 256)
    else:
        kernel, shape = (lambda *refs: merge_last_kernel(rolled, *refs)), (8, 256)
        parts.append(own)
    return pl.pallas_call(
        kernel,
        in_specs=[VMEM] * len(parts),
        out_specs=VMEM,
        out_shape=jax.ShapeDtypeStruct(shape, f32),
        compiler_params=pltpu.CompilerParams(vmem_limit_bytes=4 * 1024 * 1024),
    )(*parts)


def sums_kernel(place_ref, p0_ref, p1_ref, w_ref, x0_ref, x1_ref, keep_ref, send_ref, parts, turned):
    core, zh = place_ref[0], place_ref[1]
    first = p0_ref.shape[0]
    for tile in range(4):
        span = slice(256 * tile, 256 * tile + 256)
        count = jnp.zeros((256, 128), f32)
        for i in range(8):
            p = p0_ref[i, span, :] if i < first else p1_ref[i - first, span, :]
            soft = p * w_ref[i : i + 1, :]
            high = soft.astype(bf16)
            parts[0:256, 256 * i : 256 * i + 256] = high
            parts[256:512, 256 * i : 256 * i + 256] = (soft - high.astype(f32)).astype(bf16)
            count = count + (soft[:, :128] + soft[:, 128:])
        both = jnp.dot(parts[:, : 256 * first], x0_ref[...], preferred_element_type=f32)
        both = both + jnp.dot(parts[:, 256 * first :], x1_ref[...], preferred_element_type=f32)
        turned[...] = (both[:256] + both[256:]).T
        counted = jnp.broadcast_to(jnp.sum(count.T, axis=0, keepdims=True), (8, 256))
        if tile < 2:
            block, col = 1 - zh, jnp.bitwise_xor(core, tile)
        else:
            block, col = zh, tile - 2
        lanes = pl.ds(pl.multiple_of(col * 256, 256), 256)
        for ref, half in ((keep_ref, core), (send_ref, 1 - core)):
            for q in range(4):
                part = turned[pl.ds(pl.multiple_of(384 * half + 96 * q, 32), 96), :]
                ref[block, q, 0:96, lanes] = part
                ref[block, q, 96:104, lanes] = counted


def weighted_sums(place, ps, w, xs):
    rows = 2048
    shape = jax.ShapeDtypeStruct((2, 4, 104, 512), f32)
    return pl.pallas_call(
        sums_kernel,
        in_specs=[pl.BlockSpec(memory_space=pltpu.SMEM)] + [VMEM] * 5,
        out_specs=(VMEM, VMEM),
        out_shape=(shape, shape),
        scratch_shapes=[pltpu.VMEM((512, rows), bf16), pltpu.VMEM((D, 256), f32)],
        cost_estimate=pl.CostEstimate(
            flops=8 * rows * 512 * D,
            transcendentals=0,
            bytes_accessed=2 * rows * D + 8 * rows * 512 + 8 * 832 * 512,
        ),
        compiler_params=pltpu.CompilerParams(vmem_limit_bytes=SUMS_MB * 1024 * 1024),
    )(place, *ps, w, *xs)


def coarse_kernel(pooled_ref, parents_ref, out_ref):
    ids = lax.broadcasted_iota(jnp.int32, (KC, 512), 0)
    hot = (ids == parents_ref[...]).astype(f32).astype(bf16)
    pooled = pooled_ref[...]
    high = pooled.astype(bf16)
    low = (pooled - high.astype(f32)).astype(bf16)
    both = lax.dot_general(
        hot,
        jnp.concatenate([high, low]),
        (((1,), (1,)), ((), ())),
        preferred_element_type=f32,
    )
    out_ref[...] = both[:, :128] + both[:, 128:]


def gathered_over(tile, axis):
    size = AXES[axis]
    me = lax.axis_index(axis)
    parts = [tile] + [from_ahead(tile, axis, s) for s in range(1, size)]
    stacked = jnp.stack(parts + parts)
    return lax.dynamic_slice_in_dim(stacked, (size - me) % size, size, 0)


def joined_kernel(place_ref, *refs):
    parts, out_ref, rows = refs[:4], refs[4], refs[5]
    core, zl = place_ref[0], place_ref[2]
    for s in range(4):
        for c in (0, 1):
            piece = parts[s][c]
            at = jnp.bitwise_xor(core, c) * 4 + jnp.bitwise_and(zl + s, 3)
            rows[pl.ds(pl.multiple_of(at * 96, 32), 96), :] = piece.T[0:96]
    out_ref[...] = rows[...].T


def joined(place, parts):
    return pl.pallas_call(
        joined_kernel,
        in_specs=[pl.BlockSpec(memory_space=pltpu.SMEM)] + [VMEM] * 4,
        out_specs=VMEM,
        out_shape=jax.ShapeDtypeStruct((64, D), f32),
        scratch_shapes=[pltpu.VMEM((D, 64), f32)],
        compiler_params=pltpu.CompilerParams(vmem_limit_bytes=8 * 1024 * 1024),
    )(place, *parts)


def step(embeddings, fine, parents, coarse):
    core, zl, zh = (lax.axis_index(a) for a in ("core", "zl", "zh"))
    place = jnp.stack([core, zh, zl])

    own_narrow = fine.astype(bf16)
    own_norm = 0.5 * jnp.sum(fine * fine, axis=1)
    norm_part = lax.dynamic_slice_in_dim(own_norm, 256 * core, 256)
    parts = []
    for _ in range(3):
        parts.append(lax.reduce_precision(norm_part, 8, 7))
        norm_part = norm_part - parts[-1]
    last = jnp.broadcast_to(jnp.concatenate(parts).astype(bf16)[None], (8, D))
    share = jnp.concatenate([lax.dynamic_slice_in_dim(own_narrow, 256 * core, 256, 0), last])
    direct = from_ahead(share, "zh", 1)
    relayed = from_ahead(direct, "core", 1)
    cs = (direct, relayed, own_narrow)

    halves = (embeddings[:64], embeddings[64:])
    near = [jnp.concatenate(ring_of_four(h, axis)) for h, axis in zip(halves, ("x", "y"))]
    ahead = [from_ahead(b, axis, 1) for b, axis in zip(near, ("y", "x"))]
    behind = [from_ahead(b, axis, 3) for b, axis in zip(near, ("y", "x"))]
    far = [from_ahead(a, axis, 1) for a, axis in zip(ahead, ("y", "x"))]
    first = [near[0], ahead[0], behind[0], near[1], ahead[1], behind[1]]
    p0, stat, x0 = weigh(place, 0, (), first, cs, own_norm[None])
    p1, stat, x1 = weigh(place, 6, (stat,), far, cs, own_norm[None])
    weight = merged_over(merged_over(stat, "x", 0), "y", 1, own=stat)
    keep, send = weighted_sums(place, (p0, p1), weight, (x0, x1))
    tiles = (keep + from_ahead(send, "core", 1).astype(f32)) * SENT_SCALE
    arrived = lax.all_to_all(
        tiles.astype(f16).reshape(8, 104, 512), ("zh", "zl"), 0, 0, tiled=True
    )
    owned = jnp.sum(arrived.astype(f32), axis=0) / SENT_SCALE
    mass = 1.0 + owned[96:97]
    first_row = core * 384 + zl * 96
    pooled = lax.dynamic_slice_in_dim(fine, first_row, 96, 1).T + owned[:96]

    new_half = gathered_over((pooled / mass).astype(f16), "zl").reshape(384, 512)
    new_fine = gathered_over(new_half, "core").reshape(768, 512)
    new_fine = new_fine.astype(f32).T

    with_mass = jnp.concatenate([pooled, jnp.broadcast_to(mass, (32, 512))]) * SENT_SCALE
    part = pl.pallas_call(
        coarse_kernel,
        out_shape=jax.ShapeDtypeStruct((KC, 128), f32),
        compiler_params=pltpu.CompilerParams(vmem_limit_bytes=24 * 1024 * 1024),
    )(with_mass, parents[None])
    arrived = lax.all_to_all(
        part.astype(f16).reshape(32, 64, 128), ("y", "zh", "x"), 0, 0, tiled=True
    )
    total = jnp.sum(arrived.astype(f32), axis=0) / SENT_SCALE
    old = lax.dynamic_slice_in_dim(coarse, first_row, 96, 1)
    new_cols = (PRIOR * old + total[:, :96]) / (PRIOR + total[:, 96:97])
    cols = jnp.concatenate([new_cols, jnp.zeros((64, 32), f32)], axis=1)
    pair = jnp.stack([cols, from_ahead(cols, "core", 1)])
    parts = [pair] + [from_ahead(pair, "zl", s) for s in (1, 2, 3)]
    new_coarse = joined(place, parts)
    return new_fine, new_coarse


def solution(mesh):
    places = Mesh(mesh.devices.reshape(tuple(AXES.values())), tuple(AXES))
    cent = ("y", "zh", "x")
    in_specs = (P(("zl", "core", *cent), None), P(cent, None), P(cent), P(cent, None))
    out_specs = (P(cent, None), P(cent, None))
    return jax.shard_map(step, mesh=places, in_specs=in_specs, out_specs=out_specs, check_vma=False)
```

time: 387 us -> 158 us (0.41)
  waiting for transfers between devices: 212 us -> 57.4 us
  blocking collectives: 74.4 us -> 0 us
  starting transfers between devices: 5.35 us -> 70.7 us
  matrix products: 54.4 us -> 0 us
  Pallas kernels: 0 us -> 17.7 us
  between operations: 14.4 us -> 0.97 us
  other arithmetic: 15.7 us -> 6.82 us
  local copies, waits for them, and re-layouts: 9.1 us -> 4.14 us
    all_gather x1 -> x0, waiting for transfers between devices: 136 us -> none  [local(): gathered = lax.all_gather(embeddings, 'cent', axis=0, tiled=True)]
    ppermute x0 -> x29, starting transfers between devices: none -> 57.9 us  [the longest x11 35.6 us: from_ahead(): lax.ppermute(array, axis, [((me + step) % size, me) for me in range(size)])]
    psum x1 -> x0, waiting for transfers between devices: 56.4 us -> none  [local(): total_sums, total_counts = lax.psum((fine_sums, fine_counts), 'dp')]
    dot_general x24 -> x0, matrix products: 54.4 us -> none  [the longest x16 29 us: block_logits(): lax.dot_general(one_block, narrow_centroids, (((1,), (1,)), ((), ())), pr...]
    all_to_all x2 -> x0, blocking collectives: 51.7 us -> none  [the longest x1 36.6 us: summed_on_arrival(): lax.all_to_all(tiles, axis, split_axis=0, concat_axis=0, tiled=True)]
    ppermute x0 -> x29, waiting for transfers between devices: none -> 24.2 us  [the longest x18 15.1 us: from_ahead(): return lax.ppermute(array, ('core', axis), pairs)]
    psum x1 -> x0, blocking collectives: 22.7 us -> none  [local(): total_sums, total_counts = lax.psum((fine_sums, fine_counts), 'dp')]
    pallas_call x0 -> x7, Pallas kernels: none -> 17.7 us  [the longest x1 8.13 us: weighted_sums(): pl.pallas_call(sums_kernel, in_specs=[pl.BlockSpec(memory_space=pltpu.SME...]
  transfers between devices with their start and end apart: 3 -> 31, of which waited for: 3 -> 17; matrix products, arithmetic and copies ran while one was open for 2% -> 5% of each run, Pallas kernels for 0% -> 3%
where the time goes in v1:
time: 158 us
  starting transfers between devices  70.7 us (45%)
  waiting for transfers between devices  57.4 us (36%)
  Pallas kernels  17.7 us (11%)
  other arithmetic  6.82 us (4%)
  local copies, waits for them, and re-layouts  4.14 us (3%)
    ppermute x11, starting transfers between devices, from_ahead(): lax.ppermute(array, axis, [((me + step) % size, me) for me in range(size)])  35.6 us
    all_to_all x1, waiting for transfers between devices, step(): lax.all_to_all(tiles.astype(f16).reshape(8, 104, 512), ('zh', 'zl'), 0, 0...  23.6 us
    ppermute x18, starting transfers between devices, from_ahead(): return lax.ppermute(array, ('core', axis), pairs)  22.3 us
    ppermute x18, waiting for transfers between devices, from_ahead(): return lax.ppermute(array, ('core', axis), pairs)  15.1 us
    all_to_all x1, waiting for transfers between devices, step(): lax.all_to_all(part.astype(f16).reshape(32, 64, 128), ('y', 'zh', 'x'), 0...  9.62 us
    ppermute x11, waiting for transfers between devices, from_ahead(): lax.ppermute(array, axis, [((me + step) % size, me) for me in range(size)])  9.02 us
    pallas_call x1, Pallas kernels, weighted_sums(): pl.pallas_call(sums_kernel, in_specs=[pl.BlockSpec(memory_space=pltpu.SME...  8.13 us
    all_to_all x1, starting transfers between devices, step(): lax.all_to_all(tiles.astype(f16).reshape(8, 104, 512), ('zh', 'zl'), 0, 0...  7.61 us
  transfers between devices with their start and end apart: 31, of which 17 were waited for; matrix products, arithmetic and copies ran while one was open for 5% of the time, Pallas kernels for 3%

profile of v1, /device:TPU:1, one launch (start us, length us, event | category | flops | bytes accessed | tf_op | source)
XLA Modules:
  0.0 157.7 jit_solution(12573524447482543727)
XLA Ops:
  0.6 1.0 fusion.8
  1.6 2.2 %collective-permute-start.5 = (bf16[64,768]{1,0:T(8,128)(2,1)S(1)}, bf16[64,768]{1,0:T(8,128)(2,1)S(1)}, u32[]{:S(2)}, u32[]{:S(2)}) collective-permute-start(bf16[64,768]{1,0:T(8,128)(2,1)S(1)} %get-tuple-element.23), channel_id=1, source_target_pairs={{8,0},{16,8},{24,16},{0,24},{56,32},{32,40},{40,48},{48,56},{9,1},... | collective-permute-start | bytes 294920 | tf_op jit(solution)/shard_map/ppermute | solution.py:33
  3.8 2.6 %collective-permute-start.6 = (bf16[64,768]{1,0:T(8,128)(2,1)S(1)}, bf16[64,768]{1,0:T(8,128)(2,1)S(1)}, u32[]{:S(2)}, u32[]{:S(2)}) collective-permute-start(bf16[64,768]{1,0:T(8,128)(2,1)S(1)} %get-tuple-element.23), channel_id=1, source_target_pairs={{16,0},{24,8},{0,16},{8,24},{48,32},{56,40},{32,48},{40,56},{17,1}... | collective-permute-start | bytes 294920 | tf_op jit(solution)/shard_map/ppermute | solution.py:33
  6.4 1.1 collective-permute-start.7
  7.5 2.1 %fusion.7 = (bf16[512,768]{1,0:T(8,128)(2,1)S(1)}, f32[512]{0:T(512)S(1)}) fusion(f32[512,768]{1,0:T(8,128)} %param.5), kind=kLoop, calls=%fused_computation.47 | loop fusion | flops 1179136 | bytes 2361344 | tf_op jit(solution)/shard_map/convert_element_type | solution.py:243
  9.6 0.1 reduce-precision_convert_fusion.1
  9.8 7.0 %collective-permute-start.10 = (bf16[264,768]{1,0:T(8,128)(2,1)S(1)}, bf16[264,768]{1,0:T(8,128)(2,1)S(1)}, u32[]{:S(2)}, u32[]{:S(2)}) collective-permute-start(bf16[264,768]{1,0:T(8,128)(2,1)S(1)} %pad_maximum_fusion), channel_id=1, source_target_pairs={{4,0},{0,4},{5,1},{1,5},{6,2},{2,6},{7,3},{3,7},{12,8},{8,12},{13,... | collective-permute-start | bytes 1216520 | tf_op jit(solution)/shard_map/ppermute | solution.py:27
  16.8 1.2 collective-permute-start
  18.0 2.5 %collective-permute-start.1 = (bf16[64,768]{1,0:T(8,128)(2,1)S(1)}, bf16[64,768]{1,0:T(8,128)(2,1)S(1)}, u32[]{:S(2)}, u32[]{:S(2)}) collective-permute-start(bf16[64,768]{1,0:T(8,128)(2,1)S(1)} %get-tuple-element.24), channel_id=1, source_target_pairs={{2,0},{3,1},{0,2},{1,3},{34,32},{35,33},{32,34},{33,35},{6,4},{7,5... | collective-permute-start | bytes 294920 | tf_op jit(solution)/shard_map/ppermute | solution.py:33
  20.5 1.2 collective-permute-start.2
  21.7 0.4 collective-permute-start.8
  22.1 1.8 %collective-permute-done.1 = bf16[64,768]{1,0:T(8,128)(2,1)S(1)} collective-permute-done((bf16[64,768]{1,0:T(8,128)(2,1)S(1)}, bf16[64,768]{1,0:T(8,128)(2,1)S(1)}, u32[]{:S(2)}, u32[]{:S(2)}) %collective-permute-start.1) | collective-permute-done | bytes 98336 | tf_op jit(solution)/shard_map/ppermute | solution.py:33
  23.8 1.3 collective-permute-done.2
  25.1 0.6 collective-permute-start.3
  25.7 1.5 collective-permute-done.10.refs_7_.refs_4_
  27.3 7.1 %collective-permute-start.11 = (bf16[264,768]{1,0:T(8,128)(2,1)S(1)}, bf16[264,768]{1,0:T(8,128)(2,1)S(1)}, u32[]{:S(2)}, u32[]{:S(2)}) collective-permute-start(bf16[264,768]{1,0:T(8,128)(2,1)S(1)} %collective-permute-done.10.refs_7_.refs_4_), channel_id=1, source_target_pairs={{32,0},{0,32},{33,1},{1,33},{34,2},{2,34},{35,3},{3,35},{36,4},{4,... | collective-permute-start | bytes 1216520 | tf_op jit(solution)/shard_map/ppermute | solution.py:27
  34.4 2.5 %collective-permute-start.9 = (bf16[256,768]{1,0:T(8,128)(2,1)S(1)}, bf16[256,768]{1,0:T(8,128)(2,1)}, u32[]{:S(2)}, u32[]{:S(2)}) collective-permute-start(bf16[256,768]{1,0:T(8,128)(2,1)S(1)} %pad_maximum_fusion.2.refs_4_), channel_id=1, source_target_pairs={{3,0},{0,1},{1,2},{2,3},{33,32},{34,33},{35,34},{32,35},{7,4},{4,5... | collective-permute-start | bytes 1179656 | tf_op jit(solution)/shard_map/ppermute | solution.py:33
  36.9 1.7 %collective-permute-start.12 = (bf16[256,768]{1,0:T(8,128)(2,1)S(1)}, bf16[256,768]{1,0:T(8,128)(2,1)}, u32[]{:S(2)}, u32[]{:S(2)}) collective-permute-start(bf16[256,768]{1,0:T(8,128)(2,1)S(1)} %collective-permute-done.3.refs_2_), channel_id=1, source_target_pairs={{8,0},{16,8},{24,16},{0,24},{56,32},{32,40},{40,48},{48,56},{9,1},... | collective-permute-start | bytes 1179656 | tf_op jit(solution)/shard_map/ppermute | solution.py:33
  38.7 5.5 %collective-permute-done.9.refs_6_ = bf16[256,768]{1,0:T(8,128)(2,1)} collective-permute-done((bf16[256,768]{1,0:T(8,128)(2,1)S(1)}, bf16[256,768]{1,0:T(8,128)(2,1)}, u32[]{:S(2)}, u32[]{:S(2)}) %collective-permute-start.9) | collective-permute-done | bytes 393248 | tf_op jit(solution)/shard_map/ppermute | solution.py:33
  44.2 2.0 %collective-permute-done.4.refs_3_ = bf16[256,768]{1,0:T(8,128)(2,1)} collective-permute-done((bf16[256,768]{1,0:T(8,128)(2,1)S(1)}, bf16[256,768]{1,0:T(8,128)(2,1)}, u32[]{:S(2)}, u32[]{:S(2)}) %collective-permute-start.4) | collective-permute-done | bytes 393248 | tf_op jit(solution)/shard_map/ppermute | solution.py:33
  46.2 4.6 %shard_map.59 = (f32[6,1024,256]{2,1,0:T(8,128)S(1)}, f32[2,8,256]{2,1,0:T(8,128)S(1)}, bf16[1536,768]{1,0:T(8,128)(2,1)S(1)}) custom-call(s32[3]{0:T(128)S(1)} %pad_add_fusion.refs_0_.place_ref, bf16[256,768]{1,0:T(8,128)(2,1)S(1)} %pad_maximum_fusion.1.refs_1_, bf16[256,768]{1,0:T(8,128)(2,1)S(1)} %collective-permute-done.3.refs_2_, ...), custom_call_target="tpu_custom_call" | custom-call | flops 2415919104 | bytes 10223616 | tf_op jit(solution)/shard_map/pallas_call | solution.py:81
  50.8 2.5 %shard_map.60 = (f32[2,1024,256]{2,1,0:T(8,128)S(1)}, f32[2,8,256]{2,1,0:T(8,128)S(1)}, bf16[512,768]{1,0:T(8,128)(2,1)S(1)}) custom-call(s32[3]{0:T(128)S(1)} %pad_add_fusion.refs_0_.place_ref, f32[2,8,256]{2,1,0:T(8,128)S(1)} %get-tuple-element.11.refs_1_, bf16[256,768]{1,0:T(8,128)(2,1)} %collective-permute-done.12.refs_2_, ...), custom_call_target="tpu_custom_call" | custom-call | flops 805306368 | bytes 4456448 | tf_op jit(solution)/shard_map/pallas_call | solution.py:81
  53.4 2.7 %collective-permute-start.15 = (f32[2,8,256]{2,1,0:T(8,128)S(1)}, f32[2,8,256]{2,1,0:T(8,128)S(1)}, u32[]{:S(2)}, u32[]{:S(2)}) collective-permute-start(f32[2,8,256]{2,1,0:T(8,128)S(1)} %get-tuple-element.13.refs_0_.refs_4_), channel_id=1, source_target_pairs={{2,0},{3,1},{0,2},{1,3},{34,32},{35,33},{32,34},{33,35},{6,4},{7,5... | collective-permute-start | bytes 49160 | tf_op jit(solution)/shard_map/ppermute | solution.py:33
  56.1 1.1 collective-permute-done.14.refs_1_
  57.2 0.4 collective-permute-done.15.refs_2_
  57.6 1.5 collective-permute-done.16.refs_3_
  59.0 0.1 shard_map.61.refs_0_
  59.2 1.1 collective-permute-start.17
  60.3 2.5 %collective-permute-start.19 = (f32[2,8,256]{2,1,0:T(8,128)S(1)}, f32[2,8,256]{2,1,0:T(8,128)S(1)}, u32[]{:S(2)}, u32[]{:S(2)}) collective-permute-start(f32[2,8,256]{2,1,0:T(8,128)S(1)} %shard_map.61.refs_0_), channel_id=1, source_target_pairs={{24,0},{0,8},{8,16},{16,24},{40,32},{48,40},{56,48},{32,56},{25,1}... | collective-permute-start | bytes 49160 | tf_op jit(solution)/shard_map/ppermute | solution.py:33
  62.8 0.3 collective-permute-done.17.refs_1_
  63.0 1.3 collective-permute-done.18.refs_2_
  64.4 0.1 shard_map.62.w_ref
  64.5 8.1 %shard_map.63 = (f32[2,4,104,512]{3,2,1,0:T(8,128)S(1)}, f32[2,4,104,512]{3,2,1,0:T(8,128)S(1)}) custom-call(s32[3]{0:T(128)S(1)} %pad_add_fusion.refs_0_.place_ref, f32[6,1024,256]{2,1,0:T(8,128)S(1)} %get-tuple-element.10.p0_ref, f32[2,1024,256]{2,1,0:T(8,128)S(1)} %get-tuple-element.12.p1_ref, f32[8,256]{1,0:T(8,128)S(1)} %shard_map.62.w_ref, ...), custom_call_target="tpu_custom_call" | custom-call | flops 6442450944 | bytes 14942208 | tf_op jit(solution)/shard_map/pallas_call | solution.py:179
  72.6 6.7 %collective-permute-start.20 = (f32[2,4,104,512]{3,2,1,0:T(8,128)S(1)}, f32[2,4,104,512]{3,2,1,0:T(8,128)S(1)}, u32[]{:S(2)}, u32[]{:S(2)}) collective-permute-start(f32[2,4,104,512]{3,2,1,0:T(8,128)S(1)} %get-tuple-element.17), channel_id=1, source_target_pairs={{32,0},{0,32},{33,1},{1,33},{34,2},{2,34},{35,3},{3,35},{36,4},{4,... | collective-permute-start | bytes 5111816 | tf_op jit(solution)/shard_map/ppermute | solution.py:27
  79.4 3.2 %collective-permute-done.20 = f32[2,4,104,512]{3,2,1,0:T(8,128)S(1)} collective-permute-done((f32[2,4,104,512]{3,2,1,0:T(8,128)S(1)}, f32[2,4,104,512]{3,2,1,0:T(8,128)S(1)}, u32[]{:S(2)}, u32[]{:S(2)}) %collective-permute-start.20) | collective-permute-done | bytes 1703968 | tf_op jit(solution)/shard_map/ppermute | solution.py:27
  82.6 1.4 multiply_convert_fusion
  83.9 7.6 %all-to-all-start = ((f16[8,104,512]{2,1,0:T(8,128)(2,1)}), f16[8,104,512]{2,1,0:T(8,128)(2,1)S(1)}, u32[]{:S(2)}, u32[]{:S(2)}) async-start(f16[8,104,512]{2,1,0:T(8,128)(2,1)} %bitcast.5), calls=%async_computation | async-start | bytes 1703936 | tf_op jit(solution)/shard_map/all_to_all | solution.py:267
  91.5 1.2 constant_dynamic-slice_fusion.2
  92.7 0.1 copy.9
  92.9 23.6 %all-to-all-done = f16[8,104,512]{2,1,0:T(8,128)(2,1)S(1)} async-done(((f16[8,104,512]{2,1,0:T(8,128)(2,1)}), f16[8,104,512]{2,1,0:T(8,128)(2,1)S(1)}, u32[]{:S(2)}, u32[]{:S(2)}) %all-to-all-start) | async-done | bytes 852000 | tf_op jit(solution)/shard_map/all_to_all | solution.py:267
  116.5 0.1 convert_reduce_fusion
  116.7 0.1 collective-permute-start.21
  116.8 0.4 collective-permute-start.22
  117.3 1.0 collective-permute-start.23
  118.3 0.7 shard_map.64
  119.1 0.9 convert_element_type.32
  119.9 5.2 %all-to-all-start.1 = ((f16[32,64,128]{2,1,0:T(8,128)(2,1)}), f16[32,64,128]{2,1,0:T(8,128)(2,1)S(1)}, u32[]{:S(2)}, u32[]{:S(2)}) async-start(f16[32,64,128]{2,1,0:T(8,128)(2,1)} %bitcast.17), calls=%async_computation.1 | async-start | bytes 1048576 | tf_op jit(solution)/shard_map/all_to_all | solution.py:285
  125.2 1.7 %collective-permute-done.22 = f16[96,512]{1,0:T(8,128)(2,1)S(1)} collective-permute-done((f16[96,512]{1,0:T(8,128)(2,1)S(1)}, f16[96,512]{1,0:T(8,128)(2,1)S(1)}, u32[]{:S(2)}, u32[]{:S(2)}) %collective-permute-start.22) | collective-permute-done | bytes 98336 | tf_op jit(solution)/shard_map/ppermute | solution.py:27
  127.1 1.6 %collective-permute-start.24 = (f16[384,512]{1,0:T(8,128)(2,1)S(1)}, f16[384,512]{1,0:T(8,128)(2,1)S(1)}, u32[]{:S(2)}, u32[]{:S(2)}) collective-permute-start(f16[384,512]{1,0:T(8,128)(2,1)S(1)} %bitcast.37), channel_id=1, source_target_pairs={{32,0},{0,32},{33,1},{1,33},{34,2},{2,34},{35,3},{3,35},{36,4},{4,... | collective-permute-start | bytes 1179656 | tf_op jit(solution)/shard_map/ppermute | solution.py:27
  128.7 9.6 %all-to-all-done.1 = f16[32,64,128]{2,1,0:T(8,128)(2,1)S(1)} async-done(((f16[32,64,128]{2,1,0:T(8,128)(2,1)}), f16[32,64,128]{2,1,0:T(8,128)(2,1)S(1)}, u32[]{:S(2)}, u32[]{:S(2)}) %all-to-all-start.1) | async-done | bytes 524320 | tf_op jit(solution)/shard_map/all_to_all | solution.py:285
  138.3 0.1 convert_reduce_fusion.1
  138.4 0.2 fusion.3
  138.6 0.9 fusion.4
  139.5 5.0 %collective-permute-start.25 = (f32[64,128]{1,0:T(8,128)S(1)}, f32[64,128]{1,0:T(8,128)S(1)}, u32[]{:S(2)}, u32[]{:S(2)}) collective-permute-start(f32[64,128]{1,0:T(8,128)S(1)} %get-tuple-element.26), channel_id=1, source_target_pairs={{32,0},{0,32},{33,1},{1,33},{34,2},{2,34},{35,3},{3,35},{36,4},{4,... | collective-permute-start | bytes 98312 | tf_op jit(solution)/shard_map/ppermute | solution.py:27
  144.5 0.5 fusion.2
  145.1 0.3 collective-permute-done.25
  145.4 2.7 %collective-permute-start.26 = (f32[2,64,128]{2,1,0:T(8,128)S(1)}, f32[2,64,128]{2,1,0:T(8,128)S(1)}, u32[]{:S(2)}, u32[]{:S(2)}) collective-permute-start(f32[2,64,128]{2,1,0:T(8,128)S(1)} %pad_maximum_fusion.3.refs_0_), channel_id=1, source_target_pairs={{64,0},{128,64},{192,128},{0,192},{65,1},{129,65},{193,129},{1,193... | collective-permute-start | bytes 196616 | tf_op jit(solution)/shard_map/ppermute | solution.py:27
  148.1 2.6 %collective-permute-start.27 = (f32[2,64,128]{2,1,0:T(8,128)S(1)}, f32[2,64,128]{2,1,0:T(8,128)S(1)}, u32[]{:S(2)}, u32[]{:S(2)}) collective-permute-start(f32[2,64,128]{2,1,0:T(8,128)S(1)} %pad_maximum_fusion.3.refs_0_), channel_id=1, source_target_pairs={{128,0},{192,64},{0,128},{64,192},{129,1},{193,65},{1,129},{65,193... | collective-permute-start | bytes 196616 | tf_op jit(solution)/shard_map/ppermute | solution.py:27
  150.7 1.3 collective-permute-start.28
  152.0 0.3 bitcast_convert_fusion
  152.2 1.6 %copy.8 = f32[768,512]{0,1:T(8,128)} copy(f32[768,512]{1,0:T(8,128)S(1)} %bitcast_convert_fusion) | data formatting | bytes 3145728 | tf_op jit(solution)/shard_map/transpose | solution.py:277
  153.9 0.1 collective-permute-done.27.refs_2_
  154.0 2.2 %collective-permute-done.28.refs_3_ = f32[2,64,128]{2,1,0:T(8,128)S(1)} collective-permute-done((f32[2,64,128]{2,1,0:T(8,128)S(1)}, f32[2,64,128]{2,1,0:T(8,128)S(1)}, u32[]{:S(2)}, u32[]{:S(2)}) %collective-permute-start.28) | collective-permute-done | bytes 65568 | tf_op jit(solution)/shard_map/ppermute | solution.py:27
  156.2 1.5 shard_map.65
  (45 shorter events, 0.7 us)
Async XLA Ops:
  1.6 16.4 %collective-permute-start.5 = (bf16[64,768]{1,0:T(8,128)(2,1)S(1)}, bf16[64,768]{1,0:T(8,128)(2,1)S(1)}, u32[]{:S(2)}, u32[]{:S(2)}) collective-permute-start(bf16[64,768]{1,0:T(8,128)(2,1)S(1)} %get-tuple-element.23), channel_id=1, source_target_pairs={{8,0},{16,8},{24,16},{0,24},{56,32},{32,40},{40,48},{48,56},{9,1},... | collective-permute-start | bytes 294920 | tf_op jit(solution)/shard_map/ppermute | solution.py:33
  3.8 16.7 %collective-permute-start.6 = (bf16[64,768]{1,0:T(8,128)(2,1)S(1)}, bf16[64,768]{1,0:T(8,128)(2,1)S(1)}, u32[]{:S(2)}, u32[]{:S(2)}) collective-permute-start(bf16[64,768]{1,0:T(8,128)(2,1)S(1)} %get-tuple-element.23), channel_id=1, source_target_pairs={{16,0},{24,8},{0,16},{8,24},{48,32},{56,40},{32,48},{40,56},{17,1}... | collective-permute-start | bytes 294920 | tf_op jit(solution)/shard_map/ppermute | solution.py:33
  6.4 15.2 %collective-permute-start.7 = (bf16[64,768]{1,0:T(8,128)(2,1)S(1)}, bf16[64,768]{1,0:T(8,128)(2,1)S(1)}, u32[]{:S(2)}, u32[]{:S(2)}) collective-permute-start(bf16[64,768]{1,0:T(8,128)(2,1)S(1)} %get-tuple-element.23), channel_id=1, source_target_pairs={{24,0},{0,8},{8,16},{16,24},{40,32},{48,40},{56,48},{32,56},{25,1}... | collective-permute-start | bytes 294920 | tf_op jit(solution)/shard_map/ppermute | solution.py:33
  9.8 17.5 %collective-permute-start.10 = (bf16[264,768]{1,0:T(8,128)(2,1)S(1)}, bf16[264,768]{1,0:T(8,128)(2,1)S(1)}, u32[]{:S(2)}, u32[]{:S(2)}) collective-permute-start(bf16[264,768]{1,0:T(8,128)(2,1)S(1)} %pad_maximum_fusion), channel_id=1, source_target_pairs={{4,0},{0,4},{5,1},{1,5},{6,2},{2,6},{7,3},{3,7},{12,8},{8,12},{13,... | collective-permute-start | bytes 1216520 | tf_op jit(solution)/shard_map/ppermute | solution.py:27
  16.8 5.2 %collective-permute-start = (bf16[64,768]{1,0:T(8,128)(2,1)S(1)}, bf16[64,768]{1,0:T(8,128)(2,1)S(1)}, u32[]{:S(2)}, u32[]{:S(2)}) collective-permute-start(bf16[64,768]{1,0:T(8,128)(2,1)S(1)} %get-tuple-element.24), channel_id=1, source_target_pairs={{1,0},{2,1},{3,2},{0,3},{35,32},{32,33},{33,34},{34,35},{5,4},{6,5... | collective-permute-start | bytes 294920 | tf_op jit(solution)/shard_map/ppermute | solution.py:33
  18.0 5.8 %collective-permute-start.1 = (bf16[64,768]{1,0:T(8,128)(2,1)S(1)}, bf16[64,768]{1,0:T(8,128)(2,1)S(1)}, u32[]{:S(2)}, u32[]{:S(2)}) collective-permute-start(bf16[64,768]{1,0:T(8,128)(2,1)S(1)} %get-tuple-element.24), channel_id=1, source_target_pairs={{2,0},{3,1},{0,2},{1,3},{34,32},{35,33},{32,34},{33,35},{6,4},{7,5... | collective-permute-start | bytes 294920 | tf_op jit(solution)/shard_map/ppermute | solution.py:33
  20.5 4.6 %collective-permute-start.2 = (bf16[64,768]{1,0:T(8,128)(2,1)S(1)}, bf16[64,768]{1,0:T(8,128)(2,1)S(1)}, u32[]{:S(2)}, u32[]{:S(2)}) collective-permute-start(bf16[64,768]{1,0:T(8,128)(2,1)S(1)} %get-tuple-element.24), channel_id=1, source_target_pairs={{3,0},{0,1},{1,2},{2,3},{33,32},{34,33},{35,34},{32,35},{7,4},{4,5... | collective-permute-start | bytes 294920 | tf_op jit(solution)/shard_map/ppermute | solution.py:33
  21.7 15.2 %collective-permute-start.8 = (bf16[256,768]{1,0:T(8,128)(2,1)S(1)}, bf16[256,768]{1,0:T(8,128)(2,1)S(1)}, u32[]{:S(2)}, u32[]{:S(2)}) collective-permute-start(bf16[256,768]{1,0:T(8,128)(2,1)S(1)} %pad_maximum_fusion.2.refs_4_), channel_id=1, source_target_pairs={{1,0},{2,1},{3,2},{0,3},{35,32},{32,33},{33,34},{34,35},{5,4},{6,5... | collective-permute-start | bytes 1179656 | tf_op jit(solution)/shard_map/ppermute | solution.py:33
  25.1 11.8 %collective-permute-start.3 = (bf16[256,768]{1,0:T(8,128)(2,1)S(1)}, bf16[256,768]{1,0:T(8,128)(2,1)S(1)}, u32[]{:S(2)}, u32[]{:S(2)}) collective-permute-start(bf16[256,768]{1,0:T(8,128)(2,1)S(1)} %pad_maximum_fusion.1.refs_1_), channel_id=1, source_target_pairs={{8,0},{16,8},{24,16},{0,24},{56,32},{32,40},{40,48},{48,56},{9,1},... | collective-permute-start | bytes 1179656 | tf_op jit(solution)/shard_map/ppermute | solution.py:33
  27.3 19.0 %collective-permute-start.11 = (bf16[264,768]{1,0:T(8,128)(2,1)S(1)}, bf16[264,768]{1,0:T(8,128)(2,1)S(1)}, u32[]{:S(2)}, u32[]{:S(2)}) collective-permute-start(bf16[264,768]{1,0:T(8,128)(2,1)S(1)} %collective-permute-done.10.refs_7_.refs_4_), channel_id=1, source_target_pairs={{32,0},{0,32},{33,1},{1,33},{34,2},{2,34},{35,3},{3,35},{36,4},{4,... | collective-permute-start | bytes 1216520 | tf_op jit(solution)/shard_map/ppermute | solution.py:27
  34.4 9.8 %collective-permute-start.9 = (bf16[256,768]{1,0:T(8,128)(2,1)S(1)}, bf16[256,768]{1,0:T(8,128)(2,1)}, u32[]{:S(2)}, u32[]{:S(2)}) collective-permute-start(bf16[256,768]{1,0:T(8,128)(2,1)S(1)} %pad_maximum_fusion.2.refs_4_), channel_id=1, source_target_pairs={{3,0},{0,1},{1,2},{2,3},{33,32},{34,33},{35,34},{32,35},{7,4},{4,5... | collective-permute-start | bytes 1179656 | tf_op jit(solution)/shard_map/ppermute | solution.py:33
  36.9 9.3 %collective-permute-start.4 = (bf16[256,768]{1,0:T(8,128)(2,1)S(1)}, bf16[256,768]{1,0:T(8,128)(2,1)}, u32[]{:S(2)}, u32[]{:S(2)}) collective-permute-start(bf16[256,768]{1,0:T(8,128)(2,1)S(1)} %pad_maximum_fusion.1.refs_1_), channel_id=1, source_target_pairs={{24,0},{0,8},{8,16},{16,24},{40,32},{48,40},{56,48},{32,56},{25,1}... | collective-permute-start | bytes 1179656 | tf_op jit(solution)/shard_map/ppermute | solution.py:33
  36.9 13.9 %collective-permute-start.13 = (bf16[256,768]{1,0:T(8,128)(2,1)S(1)}, bf16[256,768]{1,0:T(8,128)(2,1)}, u32[]{:S(2)}, u32[]{:S(2)}) collective-permute-start(bf16[256,768]{1,0:T(8,128)(2,1)S(1)} %collective-permute-done.8.refs_5_), channel_id=1, source_target_pairs={{1,0},{2,1},{3,2},{0,3},{35,32},{32,33},{33,34},{34,35},{5,4},{6,5... | collective-permute-start | bytes 1179656 | tf_op jit(solution)/shard_map/ppermute | solution.py:33
  36.9 13.9 %collective-permute-start.12 = (bf16[256,768]{1,0:T(8,128)(2,1)S(1)}, bf16[256,768]{1,0:T(8,128)(2,1)}, u32[]{:S(2)}, u32[]{:S(2)}) collective-permute-start(bf16[256,768]{1,0:T(8,128)(2,1)S(1)} %collective-permute-done.3.refs_2_), channel_id=1, source_target_pairs={{8,0},{16,8},{24,16},{0,24},{56,32},{32,40},{40,48},{48,56},{9,1},... | collective-permute-start | bytes 1179656 | tf_op jit(solution)/shard_map/ppermute | solution.py:33
  53.3 3.9 %collective-permute-start.14 = (f32[2,8,256]{2,1,0:T(8,128)S(1)}, f32[2,8,256]{2,1,0:T(8,128)S(1)}, u32[]{:S(2)}, u32[]{:S(2)}) collective-permute-start(f32[2,8,256]{2,1,0:T(8,128)S(1)} %get-tuple-element.13.refs_0_.refs_4_), channel_id=1, source_target_pairs={{1,0},{2,1},{3,2},{0,3},{35,32},{32,33},{33,34},{34,35},{5,4},{6,5... | collective-permute-start | bytes 49160 | tf_op jit(solution)/shard_map/ppermute | solution.py:33
  53.4 4.2 %collective-permute-start.15 = (f32[2,8,256]{2,1,0:T(8,128)S(1)}, f32[2,8,256]{2,1,0:T(8,128)S(1)}, u32[]{:S(2)}, u32[]{:S(2)}) collective-permute-start(f32[2,8,256]{2,1,0:T(8,128)S(1)} %get-tuple-element.13.refs_0_.refs_4_), channel_id=1, source_target_pairs={{2,0},{3,1},{0,2},{1,3},{34,32},{35,33},{32,34},{33,35},{6,4},{7,5... | collective-permute-start | bytes 49160 | tf_op jit(solution)/shard_map/ppermute | solution.py:33
  56.1 3.0 %collective-permute-start.16 = (f32[2,8,256]{2,1,0:T(8,128)S(1)}, f32[2,8,256]{2,1,0:T(8,128)S(1)}, u32[]{:S(2)}, u32[]{:S(2)}) collective-permute-start(f32[2,8,256]{2,1,0:T(8,128)S(1)} %get-tuple-element.13.refs_0_.refs_4_), channel_id=1, source_target_pairs={{3,0},{0,1},{1,2},{2,3},{33,32},{34,33},{35,34},{32,35},{7,4},{4,5... | collective-permute-start | bytes 49160 | tf_op jit(solution)/shard_map/ppermute | solution.py:33
  59.2 3.9 %collective-permute-start.17 = (f32[2,8,256]{2,1,0:T(8,128)S(1)}, f32[2,8,256]{2,1,0:T(8,128)S(1)}, u32[]{:S(2)}, u32[]{:S(2)}) collective-permute-start(f32[2,8,256]{2,1,0:T(8,128)S(1)} %shard_map.61.refs_0_), channel_id=1, source_target_pairs={{8,0},{16,8},{24,16},{0,24},{56,32},{32,40},{40,48},{48,56},{9,1},... | collective-permute-start | bytes 49160 | tf_op jit(solution)/shard_map/ppermute | solution.py:33
  60.3 4.1 %collective-permute-start.18 = (f32[2,8,256]{2,1,0:T(8,128)S(1)}, f32[2,8,256]{2,1,0:T(8,128)S(1)}, u32[]{:S(2)}, u32[]{:S(2)}) collective-permute-start(f32[2,8,256]{2,1,0:T(8,128)S(1)} %shard_map.61.refs_0_), channel_id=1, source_target_pairs={{16,0},{24,8},{0,16},{8,24},{48,32},{56,40},{32,48},{40,56},{17,1}... | collective-permute-start | bytes 49160 | tf_op jit(solution)/shard_map/ppermute | solution.py:33
  60.3 4.1 %collective-permute-start.19 = (f32[2,8,256]{2,1,0:T(8,128)S(1)}, f32[2,8,256]{2,1,0:T(8,128)S(1)}, u32[]{:S(2)}, u32[]{:S(2)}) collective-permute-start(f32[2,8,256]{2,1,0:T(8,128)S(1)} %shard_map.61.refs_0_), channel_id=1, source_target_pairs={{24,0},{0,8},{8,16},{16,24},{40,32},{48,40},{56,48},{32,56},{25,1}... | collective-permute-start | bytes 49160 | tf_op jit(solution)/shard_map/ppermute | solution.py:33
  72.6 10.0 %collective-permute-start.20 = (f32[2,4,104,512]{3,2,1,0:T(8,128)S(1)}, f32[2,4,104,512]{3,2,1,0:T(8,128)S(1)}, u32[]{:S(2)}, u32[]{:S(2)}) collective-permute-start(f32[2,4,104,512]{3,2,1,0:T(8,128)S(1)} %get-tuple-element.17), channel_id=1, source_target_pairs={{32,0},{0,32},{33,1},{1,33},{34,2},{2,34},{35,3},{3,35},{36,4},{4,... | collective-permute-start | bytes 5111816 | tf_op jit(solution)/shard_map/ppermute | solution.py:27
  83.9 32.6 %all-to-all-start = ((f16[8,104,512]{2,1,0:T(8,128)(2,1)}), f16[8,104,512]{2,1,0:T(8,128)(2,1)S(1)}, u32[]{:S(2)}, u32[]{:S(2)}) async-start(f16[8,104,512]{2,1,0:T(8,128)(2,1)} %bitcast.5), calls=%async_computation | async-start | bytes 1703936 | tf_op jit(solution)/shard_map/all_to_all | solution.py:267
  92.7 25.6 %copy-start = (s32[512]{0:T(512)S(1)}, s32[512]{0:T(512)}, u32[]{:S(2)}) copy-start(s32[512]{0:T(512)} %param.6) | copy-start | bytes 6148
  116.7 8.4 %collective-permute-start.21 = (f16[96,512]{1,0:T(8,128)(2,1)S(1)}, f16[96,512]{1,0:T(8,128)(2,1)S(1)}, u32[]{:S(2)}, u32[]{:S(2)}) collective-permute-start(f16[96,512]{1,0:T(8,128)(2,1)S(1)} %get-tuple-element.19), channel_id=1, source_target_pairs={{64,0},{128,64},{192,128},{0,192},{65,1},{129,65},{193,129},{1,193... | collective-permute-start | bytes 294920 | tf_op jit(solution)/shard_map/ppermute | solution.py:27
  116.8 10.0 %collective-permute-start.22 = (f16[96,512]{1,0:T(8,128)(2,1)S(1)}, f16[96,512]{1,0:T(8,128)(2,1)S(1)}, u32[]{:S(2)}, u32[]{:S(2)}) collective-permute-start(f16[96,512]{1,0:T(8,128)(2,1)S(1)} %get-tuple-element.19), channel_id=1, source_target_pairs={{128,0},{192,64},{0,128},{64,192},{129,1},{193,65},{1,129},{65,193... | collective-permute-start | bytes 294920 | tf_op jit(solution)/shard_map/ppermute | solution.py:27
  117.3 9.6 %collective-permute-start.23 = (f16[96,512]{1,0:T(8,128)(2,1)S(1)}, f16[96,512]{1,0:T(8,128)(2,1)S(1)}, u32[]{:S(2)}, u32[]{:S(2)}) collective-permute-start(f16[96,512]{1,0:T(8,128)(2,1)S(1)} %get-tuple-element.19), channel_id=1, source_target_pairs={{192,0},{0,64},{64,128},{128,192},{193,1},{1,65},{65,129},{129,193... | collective-permute-start | bytes 294920 | tf_op jit(solution)/shard_map/ppermute | solution.py:27
  119.9 18.4 %all-to-all-start.1 = ((f16[32,64,128]{2,1,0:T(8,128)(2,1)}), f16[32,64,128]{2,1,0:T(8,128)(2,1)S(1)}, u32[]{:S(2)}, u32[]{:S(2)}) async-start(f16[32,64,128]{2,1,0:T(8,128)(2,1)} %bitcast.17), calls=%async_computation.1 | async-start | bytes 1048576 | tf_op jit(solution)/shard_map/all_to_all | solution.py:285
  127.1 17.4 %collective-permute-start.24 = (f16[384,512]{1,0:T(8,128)(2,1)S(1)}, f16[384,512]{1,0:T(8,128)(2,1)S(1)}, u32[]{:S(2)}, u32[]{:S(2)}) collective-permute-start(f16[384,512]{1,0:T(8,128)(2,1)S(1)} %bitcast.37), channel_id=1, source_target_pairs={{32,0},{0,32},{33,1},{1,33},{34,2},{2,34},{35,3},{3,35},{36,4},{4,... | collective-permute-start | bytes 1179656 | tf_op jit(solution)/shard_map/ppermute | solution.py:27
  139.5 5.8 %collective-permute-start.25 = (f32[64,128]{1,0:T(8,128)S(1)}, f32[64,128]{1,0:T(8,128)S(1)}, u32[]{:S(2)}, u32[]{:S(2)}) collective-permute-start(f32[64,128]{1,0:T(8,128)S(1)} %get-tuple-element.26), channel_id=1, source_target_pairs={{32,0},{0,32},{33,1},{1,33},{34,2},{2,34},{35,3},{3,35},{36,4},{4,... | collective-permute-start | bytes 98312 | tf_op jit(solution)/shard_map/ppermute | solution.py:27
  145.4 8.5 %collective-permute-start.26 = (f32[2,64,128]{2,1,0:T(8,128)S(1)}, f32[2,64,128]{2,1,0:T(8,128)S(1)}, u32[]{:S(2)}, u32[]{:S(2)}) collective-permute-start(f32[2,64,128]{2,1,0:T(8,128)S(1)} %pad_maximum_fusion.3.refs_0_), channel_id=1, source_target_pairs={{64,0},{128,64},{192,128},{0,192},{65,1},{129,65},{193,129},{1,193... | collective-permute-start | bytes 196616 | tf_op jit(solution)/shard_map/ppermute | solution.py:27
  148.1 5.9 %collective-permute-start.27 = (f32[2,64,128]{2,1,0:T(8,128)S(1)}, f32[2,64,128]{2,1,0:T(8,128)S(1)}, u32[]{:S(2)}, u32[]{:S(2)}) collective-permute-start(f32[2,64,128]{2,1,0:T(8,128)S(1)} %pad_maximum_fusion.3.refs_0_), channel_id=1, source_target_pairs={{128,0},{192,64},{0,128},{64,192},{129,1},{193,65},{1,129},{65,193... | collective-permute-start | bytes 196616 | tf_op jit(solution)/shard_map/ppermute | solution.py:27
  150.7 5.5 %collective-permute-start.28 = (f32[2,64,128]{2,1,0:T(8,128)S(1)}, f32[2,64,128]{2,1,0:T(8,128)S(1)}, u32[]{:S(2)}, u32[]{:S(2)}) collective-permute-start(f32[2,64,128]{2,1,0:T(8,128)S(1)} %pad_maximum_fusion.3.refs_0_), channel_id=1, source_target_pairs={{192,0},{0,64},{64,128},{128,192},{193,1},{1,65},{65,129},{129,193... | collective-permute-start | bytes 196616 | tf_op jit(solution)/shard_map/ppermute | solution.py:27

commit v2 on v1

--- a/solution.py
+++ b/solution.py
@@ -33,6 +33,10 @@
     return lax.ppermute(array, ("core", axis), pairs)
 
 
+def z_place(z):
+    return z % 4 * 2 + z // 4
+
+
 def ring_of_four(array, axis):
     return [array] + [from_ahead(array, axis, s) for s in (1, 2, 3)]
 
@@ -41,11 +45,11 @@
 
 
 def weigh_kernel(first, n, *refs):
-    skip = 2 if first else 1
+    skip = 1 if first else 0
     x_refs, c_refs, norm_ref = refs[skip : skip + n], refs[skip + n : skip + n + 3], refs[skip + n + 3]
     p_ref, stat_ref, x_all, norms = refs[skip + n + 4 :]
     if first:
-        stat_ref[...] = refs[1][...]
+        stat_ref[...] = refs[0][...]
     norms[512:1024, :] = jnp.broadcast_to(norm_ref[...], (128, 512)).T
     for at, c_ref in ((0, c_refs[0]), (256, c_refs[1])):
         row = c_ref[256:264, :].astype(f32)[0:1]
@@ -75,12 +79,12 @@
         stat_ref[1, first + i : first + i + 1, :] = mass
 
 
-def weigh(place, first, stats, xs, cs, norm):
+def weigh(first, stats, xs, cs, norm):
     n = len(xs)
     rows = 256 * n
     return pl.pallas_call(
         lambda *refs: weigh_kernel(first, n, *refs),
-        in_specs=[pl.BlockSpec(memory_space=pltpu.SMEM)] + [VMEM] * (len(stats) + n + 4),
+        in_specs=[VMEM] * (len(stats) + n + 4),
         out_specs=(VMEM,) * 3,
         out_shape=(
             jax.ShapeDtypeStruct((n, 1024, 256), f32),
@@ -94,7 +98,7 @@
             bytes_accessed=2 * rows * D + 2 * 1024 * D + 4 * rows * 1024,
         ),
         compiler_params=pltpu.CompilerParams(vmem_limit_bytes=WEIGH_MB * 1024 * 1024),
-    )(place, *stats, *xs, *cs, norm)
+    )(*stats, *xs, *cs, norm)
 
 
 PIECES = ((0, 1, 6, 2), (3, 4, 7, 5))
@@ -144,11 +148,12 @@
     )(*parts)
 
 
-def sums_kernel(place_ref, p0_ref, p1_ref, w_ref, x0_ref, x1_ref, keep_ref, send_ref, parts, turned):
-    core, zh = place_ref[0], place_ref[1]
+def sums_kernel(p0_ref, p1_ref, w_ref, x0_ref, x1_ref, keep_ref, send_ref, parts, turned):
+    core, zh = lax.axis_index("core"), lax.axis_index("zh")
     first = p0_ref.shape[0]
-    for tile in range(4):
-        span = slice(256 * tile, 256 * tile + 256)
+
+    def one_tile(tile, carried):
+        span = pl.ds(pl.multiple_of(256 * tile, 256), 256)
         count = jnp.zeros((256, 128), f32)
         for i in range(8):
             p = p0_ref[i, span, :] if i < first else p1_ref[i - first, span, :]
@@ -161,24 +166,26 @@
         both = both + jnp.dot(parts[:, 256 * first :], x1_ref[...], preferred_element_type=f32)
         turned[...] = (both[:256] + both[256:]).T
         counted = jnp.broadcast_to(jnp.sum(count.T, axis=0, keepdims=True), (8, 256))
-        if tile < 2:
-            block, col = 1 - zh, jnp.bitwise_xor(core, tile)
-        else:
-            block, col = zh, tile - 2
+        side = jnp.bitwise_and(tile, 1)
+        block = jnp.where(tile < 2, 1 - zh, zh)
+        col = jnp.where(tile < 2, jnp.bitwise_xor(core, side), side)
         lanes = pl.ds(pl.multiple_of(col * 256, 256), 256)
         for ref, half in ((keep_ref, core), (send_ref, 1 - core)):
             for q in range(4):
                 part = turned[pl.ds(pl.multiple_of(384 * half + 96 * q, 32), 96), :]
                 ref[block, q, 0:96, lanes] = part
                 ref[block, q, 96:104, lanes] = counted
-
-
-def weighted_sums(place, ps, w, xs):
+        return carried
+
+    lax.fori_loop(0, 4, one_tile, 0)
+
+
+def weighted_sums(ps, w, xs):
     rows = 2048
     shape = jax.ShapeDtypeStruct((2, 4, 104, 512), f32)
     return pl.pallas_call(
         sums_kernel,
-        in_specs=[pl.BlockSpec(memory_space=pltpu.SMEM)] + [VMEM] * 5,
+        in_specs=[VMEM] * 5,
         out_specs=(VMEM, VMEM),
         out_shape=(shape, shape),
         scratch_shapes=[pltpu.VMEM((512, rows), bf16), pltpu.VMEM((D, 256), f32)],
@@ -188,7 +195,7 @@
             bytes_accessed=2 * rows * D + 8 * rows * 512 + 8 * 832 * 512,
         ),
         compiler_params=pltpu.CompilerParams(vmem_limit_bytes=SUMS_MB * 1024 * 1024),
-    )(place, *ps, w, *xs)
+    )(*ps, w, *xs)
 
 
 def coarse_kernel(pooled_ref, parents_ref, out_ref):
@@ -214,9 +221,9 @@
     return lax.dynamic_slice_in_dim(stacked, (size - me) % size, size, 0)
 
 
-def joined_kernel(place_ref, *refs):
+def joined_kernel(*refs):
     parts, out_ref, rows = refs[:4], refs[4], refs[5]
-    core, zl = place_ref[0], place_ref[2]
+    core, zl = lax.axis_index("core"), lax.axis_index("zl")
     for s in range(4):
         for c in (0, 1):
             piece = parts[s][c]
@@ -225,20 +232,19 @@
     out_ref[...] = rows[...].T
 
 
-def joined(place, parts):
+def joined(parts):
     return pl.pallas_call(
         joined_kernel,
-        in_specs=[pl.BlockSpec(memory_space=pltpu.SMEM)] + [VMEM] * 4,
+        in_specs=[VMEM] * 4,
         out_specs=VMEM,
         out_shape=jax.ShapeDtypeStruct((64, D), f32),
         scratch_shapes=[pltpu.VMEM((D, 64), f32)],
         compiler_params=pltpu.CompilerParams(vmem_limit_bytes=8 * 1024 * 1024),
-    )(place, *parts)
+    )(*parts)
 
 
 def step(embeddings, fine, parents, coarse):
     core, zl, zh = (lax.axis_index(a) for a in ("core", "zl", "zh"))
-    place = jnp.stack([core, zh, zl])
 
     own_narrow = fine.astype(bf16)
     own_norm = 0.5 * jnp.sum(fine * fine, axis=1)
@@ -247,7 +253,9 @@
     for _ in range(3):
         parts.append(lax.reduce_precision(norm_part, 8, 7))
         norm_part = norm_part - parts[-1]
-    last = jnp.broadcast_to(jnp.concatenate(parts).astype(bf16)[None], (8, D))
+    place = (core + 2 * zh + 4 * zl).astype(f32)
+    is_norm = lax.broadcasted_iota(jnp.int32, (8, D), 0) == 0
+    last = jnp.where(is_norm, jnp.concatenate(parts)[None], place).astype(bf16)
     share = jnp.concatenate([lax.dynamic_slice_in_dim(own_narrow, 256 * core, 256, 0), last])
     direct = from_ahead(share, "zh", 1)
     relayed = from_ahead(direct, "core", 1)
@@ -259,15 +267,19 @@
     behind = [from_ahead(b, axis, 3) for b, axis in zip(near, ("y", "x"))]
     far = [from_ahead(a, axis, 1) for a, axis in zip(ahead, ("y", "x"))]
     first = [near[0], ahead[0], behind[0], near[1], ahead[1], behind[1]]
-    p0, stat, x0 = weigh(place, 0, (), first, cs, own_norm[None])
-    p1, stat, x1 = weigh(place, 6, (stat,), far, cs, own_norm[None])
+    p0, stat, x0 = weigh(0, (), first, cs, own_norm[None])
+    p1, stat, x1 = weigh(6, (stat,), far, cs, own_norm[None])
     weight = merged_over(merged_over(stat, "x", 0), "y", 1, own=stat)
-    keep, send = weighted_sums(place, (p0, p1), weight, (x0, x1))
+    keep, send = weighted_sums((p0, p1), weight, (x0, x1))
     tiles = (keep + from_ahead(send, "core", 1).astype(f32)) * SENT_SCALE
-    arrived = lax.all_to_all(
-        tiles.astype(f16).reshape(8, 104, 512), ("zh", "zl"), 0, 0, tiled=True
-    )
-    owned = jnp.sum(arrived.astype(f32), axis=0) / SENT_SCALE
+    tiles = tiles.astype(f16).reshape(8, 104, 512)
+    z = zh * 4 + zl
+    owned = lax.dynamic_index_in_dim(tiles, z, 0, keepdims=False).astype(f32)
+    for s in (4, 3, 5, 2, 6, 1, 7):
+        sent = lax.dynamic_index_in_dim(tiles, jnp.bitwise_and(z - s, 7), 0, keepdims=False)
+        pairs = [(z_place((me + s) % 8), z_place(me)) for me in range(8)]
+        owned = owned + lax.ppermute(sent, ("zl", "zh"), pairs).astype(f32)
+    owned = owned / SENT_SCALE
     mass = 1.0 + owned[96:97]
     first_row = core * 384 + zl * 96
     pooled = lax.dynamic_slice_in_dim(fine, first_row, 96, 1).T + owned[:96]
@@ -291,7 +303,7 @@
     cols = jnp.concatenate([new_cols, jnp.zeros((64, 32), f32)], axis=1)
     pair = jnp.stack([cols, from_ahead(cols, "core", 1)])
     parts = [pair] + [from_ahead(pair, "zl", s) for s in (1, 2, 3)]
-    new_coarse = joined(place, parts)
+    new_coarse = joined(parts)
     return new_fine, new_coarse
 
 

time: 158 us -> 154 us (0.975)
  waiting for transfers between devices: 57.4 us -> 37.2 us
  starting transfers between devices: 70.7 us -> 87.3 us
  Pallas kernels: 17.7 us -> 15.5 us
    all_to_all x1 -> x0, waiting for transfers between devices: 23.6 us -> none  [step(): lax.all_to_all(tiles.astype(f16).reshape(8, 104, 512), ('zh', 'zl'), 0, 0...]
    ppermute x0 -> x7, starting transfers between devices: none -> 21.8 us  [step(): owned = owned + lax.ppermute(sent, ('zl', 'zh'), pairs).astype(f32)]
    all_to_all x1 -> x0, starting transfers between devices: 7.61 us -> none  [step(): lax.all_to_all(tiles.astype(f16).reshape(8, 104, 512), ('zh', 'zl'), 0, 0...]
    ppermute x0 -> x7, waiting for transfers between devices: none -> 2.53 us  [step(): owned = owned + lax.ppermute(sent, ('zl', 'zh'), pairs).astype(f32)]
    pallas_call x4, Pallas kernels: 16.7 us -> 14.5 us  [the longest x1 8.73 us: weighted_sums(): pl.pallas_call(sums_kernel, in_specs=[VMEM] * 5, out_specs=(VMEM, VMEM),...]
    all_to_all x1, waiting for transfers between devices: 9.62 us -> 11.5 us  [step(): lax.all_to_all(part.astype(f16).reshape(32, 64, 128), ('y', 'zh', 'x'), 0...]
  transfers between devices with their start and end apart: 31 -> 37, of which waited for: 17 -> 17; matrix products, arithmetic and copies ran while one was open for 5% -> 6% of each run, Pallas kernels for 3% -> 3%
where the time goes in v2:
time: 154 us; the launch traced here: 153 us
  starting transfers between devices  87.3 us (57%)
  waiting for transfers between devices  37.2 us (24%)
  Pallas kernels  15.5 us (10%)
  other arithmetic  7.33 us (5%)
  local copies, waits for them, and re-layouts  4.32 us (3%)
    ppermute x11, starting transfers between devices, from_ahead(): lax.ppermute(array, axis, [((me + step) % size, me) for me in range(size)])  36.8 us
    ppermute x18, starting transfers between devices, from_ahead(): return lax.ppermute(array, ('core', axis), pairs)  22.8 us
    ppermute x7, starting transfers between devices, step(): owned = owned + lax.ppermute(sent, ('zl', 'zh'), pairs).astype(f32)  21.8 us
    ppermute x18, waiting for transfers between devices, from_ahead(): return lax.ppermute(array, ('core', axis), pairs)  14.5 us
    all_to_all x1, waiting for transfers between devices, step(): lax.all_to_all(part.astype(f16).reshape(32, 64, 128), ('y', 'zh', 'x'), 0...  11.5 us
    ppermute x11, waiting for transfers between devices, from_ahead(): lax.ppermute(array, axis, [((me + step) % size, me) for me in range(size)])  8.73 us
    pallas_call x1, Pallas kernels, weighted_sums(): pl.pallas_call(sums_kernel, in_specs=[VMEM] * 5, out_specs=(VMEM, VMEM),...  8.73 us
    all_to_all x1, starting transfers between devices, step(): lax.all_to_all(part.astype(f16).reshape(32, 64, 128), ('y', 'zh', 'x'), 0...  5.88 us
  transfers between devices with their start and end apart: 37, of which 17 were waited for; matrix products, arithmetic and copies ran while one was open for 6% of the time, Pallas kernels for 3%

profile of v2, /device:TPU:1, one launch (start us, length us, event | category | flops | bytes accessed | tf_op | source)
XLA Modules:
  0.0 152.7 jit_solution(8699664125263265895)
XLA Ops:
  0.6 1.0 fusion.14
  1.6 2.2 %collective-permute-start.5 = (bf16[64,768]{1,0:T(8,128)(2,1)S(1)}, bf16[64,768]{1,0:T(8,128)(2,1)S(1)}, u32[]{:S(2)}, u32[]{:S(2)}) collective-permute-start(bf16[64,768]{1,0:T(8,128)(2,1)S(1)} %get-tuple-element.30), channel_id=1, source_target_pairs={{8,0},{16,8},{24,16},{0,24},{56,32},{32,40},{40,48},{48,56},{9,1},... | collective-permute-start | bytes 294920 | tf_op jit(solution)/shard_map/ppermute | solution.py:33
  3.8 2.6 %collective-permute-start.6 = (bf16[64,768]{1,0:T(8,128)(2,1)S(1)}, bf16[64,768]{1,0:T(8,128)(2,1)S(1)}, u32[]{:S(2)}, u32[]{:S(2)}) collective-permute-start(bf16[64,768]{1,0:T(8,128)(2,1)S(1)} %get-tuple-element.30), channel_id=1, source_target_pairs={{16,0},{24,8},{0,16},{8,24},{48,32},{56,40},{32,48},{40,56},{17,1}... | collective-permute-start | bytes 294920 | tf_op jit(solution)/shard_map/ppermute | solution.py:33
  6.4 1.1 collective-permute-start.7
  7.5 2.1 %fusion.13 = (bf16[512,768]{1,0:T(8,128)(2,1)S(1)}, f32[512]{0:T(512)S(1)}) fusion(f32[512,768]{1,0:T(8,128)} %param.5), kind=kLoop, calls=%fused_computation.59 | loop fusion | flops 1179136 | bytes 2361344 | tf_op jit(solution)/shard_map/convert_element_type | solution.py:249
  9.9 7.0 %collective-permute-start.10 = (bf16[264,768]{1,0:T(8,128)(2,1)S(1)}, bf16[264,768]{1,0:T(8,128)(2,1)S(1)}, u32[]{:S(2)}, u32[]{:S(2)}) collective-permute-start(bf16[264,768]{1,0:T(8,128)(2,1)S(1)} %pad_maximum_fusion), channel_id=1, source_target_pairs={{4,0},{0,4},{5,1},{1,5},{6,2},{2,6},{7,3},{3,7},{12,8},{8,12},{13,... | collective-permute-start | bytes 1216520 | tf_op jit(solution)/shard_map/ppermute | solution.py:27
  16.9 1.2 collective-permute-start
  18.1 2.5 %collective-permute-start.1 = (bf16[64,768]{1,0:T(8,128)(2,1)S(1)}, bf16[64,768]{1,0:T(8,128)(2,1)S(1)}, u32[]{:S(2)}, u32[]{:S(2)}) collective-permute-start(bf16[64,768]{1,0:T(8,128)(2,1)S(1)} %get-tuple-element.31), channel_id=1, source_target_pairs={{2,0},{3,1},{0,2},{1,3},{34,32},{35,33},{32,34},{33,35},{6,4},{7,5... | collective-permute-start | bytes 294920 | tf_op jit(solution)/shard_map/ppermute | solution.py:33
  20.6 1.2 collective-permute-start.2
  21.7 0.4 collective-permute-start.8
  22.1 1.8 %collective-permute-done.1 = bf16[64,768]{1,0:T(8,128)(2,1)S(1)} collective-permute-done((bf16[64,768]{1,0:T(8,128)(2,1)S(1)}, bf16[64,768]{1,0:T(8,128)(2,1)S(1)}, u32[]{:S(2)}, u32[]{:S(2)}) %collective-permute-start.1) | collective-permute-done | bytes 98336 | tf_op jit(solution)/shard_map/ppermute | solution.py:33
  23.9 1.3 collective-permute-done.2
  25.2 0.6 collective-permute-start.3
  25.8 1.5 %collective-permute-done.10.refs_6_.refs_3_ = bf16[264,768]{1,0:T(8,128)(2,1)S(1)} collective-permute-done((bf16[264,768]{1,0:T(8,128)(2,1)S(1)}, bf16[264,768]{1,0:T(8,128)(2,1)S(1)}, u32[]{:S(2)}, u32[]{:S(2)}) %collective-permute-start.10) | collective-permute-done | bytes 405536 | tf_op jit(solution)/shard_map/ppermute | solution.py:27
  27.4 7.1 %collective-permute-start.11 = (bf16[264,768]{1,0:T(8,128)(2,1)S(1)}, bf16[264,768]{1,0:T(8,128)(2,1)S(1)}, u32[]{:S(2)}, u32[]{:S(2)}) collective-permute-start(bf16[264,768]{1,0:T(8,128)(2,1)S(1)} %collective-permute-done.10.refs_6_.refs_3_), channel_id=1, source_target_pairs={{32,0},{0,32},{33,1},{1,33},{34,2},{2,34},{35,3},{3,35},{36,4},{4,... | collective-permute-start | bytes 1216520 | tf_op jit(solution)/shard_map/ppermute | solution.py:27
  34.5 2.5 %collective-permute-start.9 = (bf16[256,768]{1,0:T(8,128)(2,1)S(1)}, bf16[256,768]{1,0:T(8,128)(2,1)S(1)}, u32[]{:S(2)}, u32[]{:S(2)}) collective-permute-start(bf16[256,768]{1,0:T(8,128)(2,1)S(1)} %pad_maximum_fusion.2.refs_3_), channel_id=1, source_target_pairs={{3,0},{0,1},{1,2},{2,3},{33,32},{34,33},{35,34},{32,35},{7,4},{4,5... | collective-permute-start | bytes 1179656 | tf_op jit(solution)/shard_map/ppermute | solution.py:33
  37.0 1.7 %collective-permute-start.12 = (bf16[256,768]{1,0:T(8,128)(2,1)S(1)}, bf16[256,768]{1,0:T(8,128)(2,1)S(1)}, u32[]{:S(2)}, u32[]{:S(2)}) collective-permute-start(bf16[256,768]{1,0:T(8,128)(2,1)S(1)} %collective-permute-done.3.refs_1_), channel_id=1, source_target_pairs={{8,0},{16,8},{24,16},{0,24},{56,32},{32,40},{40,48},{48,56},{9,1},... | collective-permute-start | bytes 1179656 | tf_op jit(solution)/shard_map/ppermute | solution.py:33
  38.7 5.6 %collective-permute-done.9.refs_5_ = bf16[256,768]{1,0:T(8,128)(2,1)S(1)} collective-permute-done((bf16[256,768]{1,0:T(8,128)(2,1)S(1)}, bf16[256,768]{1,0:T(8,128)(2,1)S(1)}, u32[]{:S(2)}, u32[]{:S(2)}) %collective-permute-start.9) | collective-permute-done | bytes 393248 | tf_op jit(solution)/shard_map/ppermute | solution.py:33
  44.3 1.9 %collective-permute-done.4.refs_2_ = bf16[256,768]{1,0:T(8,128)(2,1)S(1)} collective-permute-done((bf16[256,768]{1,0:T(8,128)(2,1)S(1)}, bf16[256,768]{1,0:T(8,128)(2,1)S(1)}, u32[]{:S(2)}, u32[]{:S(2)}) %collective-permute-start.4) | collective-permute-done | bytes 393248 | tf_op jit(solution)/shard_map/ppermute | solution.py:33
  46.2 3.4 %shard_map.59 = (f32[6,1024,256]{2,1,0:T(8,128)S(1)}, f32[2,8,256]{2,1,0:T(8,128)S(1)}, bf16[1536,768]{1,0:T(8,128)(2,1)S(1)}) custom-call(bf16[256,768]{1,0:T(8,128)(2,1)S(1)} %pad_maximum_fusion.1.refs_0_, bf16[256,768]{1,0:T(8,128)(2,1)S(1)} %collective-permute-done.3.refs_1_, bf16[256,768]{1,0:T(8,128)(2,1)S(1)} %collective-permute-done.4.refs_2_, ...), custom_call_target="tpu_custom_call" | custom-call | flops 2415919104 | bytes 10223616 | tf_op jit(solution)/shard_map/pallas_call | solution.py:85
  49.7 1.4 shard_map.60
  51.1 2.7 %collective-permute-start.15 = (f32[2,8,256]{2,1,0:T(8,128)S(1)}, f32[2,8,256]{2,1,0:T(8,128)S(1)}, u32[]{:S(2)}, u32[]{:S(2)}) collective-permute-start(f32[2,8,256]{2,1,0:T(8,128)S(1)} %get-tuple-element.13.refs_0_.refs_4_), channel_id=1, source_target_pairs={{2,0},{3,1},{0,2},{1,3},{34,32},{35,33},{32,34},{33,35},{6,4},{7,5... | collective-permute-start | bytes 49160 | tf_op jit(solution)/shard_map/ppermute | solution.py:33
  53.8 0.6 collective-permute-start.16
  54.4 0.5 collective-permute-done.14.refs_1_
  54.9 0.4 collective-permute-done.15.refs_2_
  55.3 1.5 collective-permute-done.16.refs_3_
  56.9 1.1 collective-permute-start.17
  58.0 2.5 %collective-permute-start.19 = (f32[2,8,256]{2,1,0:T(8,128)S(1)}, f32[2,8,256]{2,1,0:T(8,128)S(1)}, u32[]{:S(2)}, u32[]{:S(2)}) collective-permute-start(f32[2,8,256]{2,1,0:T(8,128)S(1)} %shard_map.61.refs_0_), channel_id=1, source_target_pairs={{24,0},{0,8},{8,16},{16,24},{40,32},{48,40},{56,48},{32,56},{25,1}... | collective-permute-start | bytes 49160 | tf_op jit(solution)/shard_map/ppermute | solution.py:33
  60.5 0.3 collective-permute-done.17.refs_1_
  60.8 1.3 collective-permute-done.18.refs_2_
  62.2 8.7 %shard_map.63 = (f32[2,4,104,512]{3,2,1,0:T(8,128)S(1)}, f32[2,4,104,512]{3,2,1,0:T(8,128)S(1)}) custom-call(f32[6,1024,256]{2,1,0:T(8,128)S(1)} %get-tuple-element.10.p0_ref, f32[2,1024,256]{2,1,0:T(8,128)S(1)} %get-tuple-element.12.p1_ref, f32[8,256]{1,0:T(8,128)S(1)} %shard_map.62.w_ref, bf16[1536,768]{1,0:T(8,128)(2,1)S(1)} %get-tuple-element.14.x0_ref, ...), custom_call_target="tpu_custom_call" | custom-call | flops 6442450944 | bytes 14942208 | tf_op jit(solution)/shard_map/pallas_call | solution.py:186
  70.9 6.7 %collective-permute-start.20 = (f32[2,4,104,512]{3,2,1,0:T(8,128)S(1)}, f32[2,4,104,512]{3,2,1,0:T(8,128)}, u32[]{:S(2)}, u32[]{:S(2)}) collective-permute-start(f32[2,4,104,512]{3,2,1,0:T(8,128)S(1)} %get-tuple-element.17), channel_id=1, source_target_pairs={{32,0},{0,32},{33,1},{1,33},{34,2},{2,34},{35,3},{3,35},{36,4},{4,... | collective-permute-start | bytes 5111816 | tf_op jit(solution)/shard_map/ppermute | solution.py:27
  77.7 3.4 %collective-permute-done.20 = f32[2,4,104,512]{3,2,1,0:T(8,128)} collective-permute-done((f32[2,4,104,512]{3,2,1,0:T(8,128)S(1)}, f32[2,4,104,512]{3,2,1,0:T(8,128)}, u32[]{:S(2)}, u32[]{:S(2)}) %collective-permute-start.20) | collective-permute-done | bytes 1703968 | tf_op jit(solution)/shard_map/ppermute | solution.py:27
  81.0 1.9 %multiply_convert_fusion = f16[2,4,104,512]{3,2,1,0:T(8,128)(2,1)S(1)} fusion(f32[2,4,104,512]{3,2,1,0:T(8,128)S(1)} %get-tuple-element.16, f32[2,4,104,512]{3,2,1,0:T(8,128)} %collective-permute-done.20), kind=kLoop, calls=%fused_computation | loop fusion | flops 1277952 | bytes 4259840 | tf_op jit(solution)/shard_map/convert_element_type | solution.py:275
  82.9 0.2 dynamic-slice_bitcast_fusion.6
  83.1 6.2 %collective-permute-start.21 = (f16[104,512]{1,0:T(8,128)(2,1)S(1)}, f16[104,512]{1,0:T(8,128)(2,1)S(1)}, u32[]{:S(2)}, u32[]{:S(2)}) collective-permute-start(f16[104,512]{1,0:T(8,128)(2,1)S(1)} %get-tuple-element.23), channel_id=1, source_target_pairs={{4,0},{68,64},{132,128},{196,192},{0,4},{64,68},{128,132},{192,196... | collective-permute-start | bytes 319496 | tf_op jit(solution)/shard_map/ppermute | solution.py:281
  89.3 0.5 collective-permute-start.22
  89.8 2.8 %collective-permute-start.23 = (f16[104,512]{1,0:T(8,128)(2,1)S(1)}, f16[104,512]{1,0:T(8,128)(2,1)S(1)}, u32[]{:S(2)}, u32[]{:S(2)}) collective-permute-start(f16[104,512]{1,0:T(8,128)(2,1)S(1)} %get-tuple-element.28), channel_id=1, source_target_pairs={{68,0},{132,64},{196,128},{0,192},{64,4},{128,68},{192,132},{4,196... | collective-permute-start | bytes 319496 | tf_op jit(solution)/shard_map/ppermute | solution.py:281
  92.6 1.4 collective-permute-start.24
  94.0 1.4 collective-permute-start.25
  95.4 2.1 %collective-permute-start.26 = (f16[104,512]{1,0:T(8,128)(2,1)S(1)}, f16[104,512]{1,0:T(8,128)(2,1)S(1)}, u32[]{:S(2)}, u32[]{:S(2)}) collective-permute-start(f16[104,512]{1,0:T(8,128)(2,1)S(1)} %get-tuple-element.25), channel_id=1, source_target_pairs={{64,0},{128,64},{192,128},{4,192},{68,4},{132,68},{196,132},{0,196... | collective-permute-start | bytes 319496 | tf_op jit(solution)/shard_map/ppermute | solution.py:281
  97.6 7.3 %collective-permute-start.27 = (f16[104,512]{1,0:T(8,128)(2,1)S(1)}, f16[104,512]{1,0:T(8,128)(2,1)S(1)}, u32[]{:S(2)}, u32[]{:S(2)}) collective-permute-start(f16[104,512]{1,0:T(8,128)(2,1)S(1)} %get-tuple-element.24), channel_id=1, source_target_pairs={{196,0},{0,64},{64,128},{128,192},{192,4},{4,68},{68,132},{132,196... | collective-permute-start | bytes 319496 | tf_op jit(solution)/shard_map/ppermute | solution.py:281
  104.9 1.2 constant_dynamic-slice_fusion.2
  106.3 0.9 collective-permute-done.26
  107.2 1.6 %collective-permute-done.27 = f16[104,512]{1,0:T(8,128)(2,1)S(1)} collective-permute-done((f16[104,512]{1,0:T(8,128)(2,1)S(1)}, f16[104,512]{1,0:T(8,128)(2,1)S(1)}, u32[]{:S(2)}, u32[]{:S(2)}) %collective-permute-start.27) | collective-permute-done | bytes 106528 | tf_op jit(solution)/shard_map/ppermute | solution.py:281
  109.0 3.0 %collective-permute-start.28 = (f16[96,512]{1,0:T(8,128)(2,1)S(1)}, f16[96,512]{1,0:T(8,128)(2,1)S(1)}, u32[]{:S(2)}, u32[]{:S(2)}) collective-permute-start(f16[96,512]{1,0:T(8,128)(2,1)S(1)} %get-tuple-element.19), channel_id=1, source_target_pairs={{64,0},{128,64},{192,128},{0,192},{65,1},{129,65},{193,129},{1,193... | collective-permute-start | bytes 294920 | tf_op jit(solution)/shard_map/ppermute | solution.py:27
  111.9 0.7 collective-permute-start.30
  112.7 0.7 shard_map.64
  113.4 0.9 convert_element_type.67
  114.3 5.9 %all-to-all-start = ((f16[32,64,128]{2,1,0:T(8,128)(2,1)}), f16[32,64,128]{2,1,0:T(8,128)(2,1)S(1)}, u32[]{:S(2)}, u32[]{:S(2)}) async-start(f16[32,64,128]{2,1,0:T(8,128)(2,1)} %bitcast.22), calls=%async_computation | async-start | bytes 1048576 | tf_op jit(solution)/shard_map/all_to_all | solution.py:297
  120.2 0.8 collective-permute-done.29
  121.3 1.0 collective-permute-start.31
  122.2 11.5 %all-to-all-done = f16[32,64,128]{2,1,0:T(8,128)(2,1)S(1)} async-done(((f16[32,64,128]{2,1,0:T(8,128)(2,1)}), f16[32,64,128]{2,1,0:T(8,128)(2,1)S(1)}, u32[]{:S(2)}, u32[]{:S(2)}) %all-to-all-start) | async-done | bytes 524320 | tf_op jit(solution)/shard_map/all_to_all | solution.py:297
  134.0 0.9 fusion.11
  134.9 3.0 %collective-permute-start.32 = (f32[64,128]{1,0:T(8,128)S(1)}, f32[64,128]{1,0:T(8,128)S(1)}, u32[]{:S(2)}, u32[]{:S(2)}) collective-permute-start(f32[64,128]{1,0:T(8,128)S(1)} %get-tuple-element.33), channel_id=1, source_target_pairs={{32,0},{0,32},{33,1},{1,33},{34,2},{2,34},{35,3},{3,35},{36,4},{4,... | collective-permute-start | bytes 98312 | tf_op jit(solution)/shard_map/ppermute | solution.py:27
  137.9 0.5 fusion.2
  138.4 0.3 collective-permute-done.32
  138.7 3.3 %collective-permute-start.33 = (f32[2,64,128]{2,1,0:T(8,128)S(1)}, f32[2,64,128]{2,1,0:T(8,128)S(1)}, u32[]{:S(2)}, u32[]{:S(2)}) collective-permute-start(f32[2,64,128]{2,1,0:T(8,128)S(1)} %pad_maximum_fusion.3.refs_0_), channel_id=1, source_target_pairs={{64,0},{128,64},{192,128},{0,192},{65,1},{129,65},{193,129},{1,193... | collective-permute-start | bytes 196616 | tf_op jit(solution)/shard_map/ppermute | solution.py:27
  142.0 4.7 %collective-permute-start.34 = (f32[2,64,128]{2,1,0:T(8,128)S(1)}, f32[2,64,128]{2,1,0:T(8,128)S(1)}, u32[]{:S(2)}, u32[]{:S(2)}) collective-permute-start(f32[2,64,128]{2,1,0:T(8,128)S(1)} %pad_maximum_fusion.3.refs_0_), channel_id=1, source_target_pairs={{128,0},{192,64},{0,128},{64,192},{129,1},{193,65},{1,129},{65,193... | collective-permute-start | bytes 196616 | tf_op jit(solution)/shard_map/ppermute | solution.py:27
  146.7 0.4 collective-permute-start.35
  147.1 0.3 bitcast_convert_fusion
  147.4 1.6 %copy.8 = f32[768,512]{0,1:T(8,128)} copy(f32[768,512]{1,0:T(8,128)S(1)} %bitcast_convert_fusion) | data formatting | bytes 3145728 | tf_op jit(solution)/shard_map/transpose | solution.py:289
  149.0 2.7 %collective-permute-done.34.refs_2_ = f32[2,64,128]{2,1,0:T(8,128)S(1)} collective-permute-done((f32[2,64,128]{2,1,0:T(8,128)S(1)}, f32[2,64,128]{2,1,0:T(8,128)S(1)}, u32[]{:S(2)}, u32[]{:S(2)}) %collective-permute-start.34) | collective-permute-done | bytes 65568 | tf_op jit(solution)/shard_map/ppermute | solution.py:27
  151.7 1.0 shard_map.65
  (57 shorter events, 1.5 us)
Async XLA Ops:
  1.6 16.5 %collective-permute-start.5 = (bf16[64,768]{1,0:T(8,128)(2,1)S(1)}, bf16[64,768]{1,0:T(8,128)(2,1)S(1)}, u32[]{:S(2)}, u32[]{:S(2)}) collective-permute-start(bf16[64,768]{1,0:T(8,128)(2,1)S(1)} %get-tuple-element.30), channel_id=1, source_target_pairs={{8,0},{16,8},{24,16},{0,24},{56,32},{32,40},{40,48},{48,56},{9,1},... | collective-permute-start | bytes 294920 | tf_op jit(solution)/shard_map/ppermute | solution.py:33
  3.8 16.8 %collective-permute-start.6 = (bf16[64,768]{1,0:T(8,128)(2,1)S(1)}, bf16[64,768]{1,0:T(8,128)(2,1)S(1)}, u32[]{:S(2)}, u32[]{:S(2)}) collective-permute-start(bf16[64,768]{1,0:T(8,128)(2,1)S(1)} %get-tuple-element.30), channel_id=1, source_target_pairs={{16,0},{24,8},{0,16},{8,24},{48,32},{56,40},{32,48},{40,56},{17,1}... | collective-permute-start | bytes 294920 | tf_op jit(solution)/shard_map/ppermute | solution.py:33
  6.4 15.3 %collective-permute-start.7 = (bf16[64,768]{1,0:T(8,128)(2,1)S(1)}, bf16[64,768]{1,0:T(8,128)(2,1)S(1)}, u32[]{:S(2)}, u32[]{:S(2)}) collective-permute-start(bf16[64,768]{1,0:T(8,128)(2,1)S(1)} %get-tuple-element.30), channel_id=1, source_target_pairs={{24,0},{0,8},{8,16},{16,24},{40,32},{48,40},{56,48},{32,56},{25,1}... | collective-permute-start | bytes 294920 | tf_op jit(solution)/shard_map/ppermute | solution.py:33
  9.9 17.5 %collective-permute-start.10 = (bf16[264,768]{1,0:T(8,128)(2,1)S(1)}, bf16[264,768]{1,0:T(8,128)(2,1)S(1)}, u32[]{:S(2)}, u32[]{:S(2)}) collective-permute-start(bf16[264,768]{1,0:T(8,128)(2,1)S(1)} %pad_maximum_fusion), channel_id=1, source_target_pairs={{4,0},{0,4},{5,1},{1,5},{6,2},{2,6},{7,3},{3,7},{12,8},{8,12},{13,... | collective-permute-start | bytes 1216520 | tf_op jit(solution)/shard_map/ppermute | solution.py:27
  16.9 5.2 %collective-permute-start = (bf16[64,768]{1,0:T(8,128)(2,1)S(1)}, bf16[64,768]{1,0:T(8,128)(2,1)S(1)}, u32[]{:S(2)}, u32[]{:S(2)}) collective-permute-start(bf16[64,768]{1,0:T(8,128)(2,1)S(1)} %get-tuple-element.31), channel_id=1, source_target_pairs={{1,0},{2,1},{3,2},{0,3},{35,32},{32,33},{33,34},{34,35},{5,4},{6,5... | collective-permute-start | bytes 294920 | tf_op jit(solution)/shard_map/ppermute | solution.py:33
  18.1 5.8 %collective-permute-start.1 = (bf16[64,768]{1,0:T(8,128)(2,1)S(1)}, bf16[64,768]{1,0:T(8,128)(2,1)S(1)}, u32[]{:S(2)}, u32[]{:S(2)}) collective-permute-start(bf16[64,768]{1,0:T(8,128)(2,1)S(1)} %get-tuple-element.31), channel_id=1, source_target_pairs={{2,0},{3,1},{0,2},{1,3},{34,32},{35,33},{32,34},{33,35},{6,4},{7,5... | collective-permute-start | bytes 294920 | tf_op jit(solution)/shard_map/ppermute | solution.py:33
  20.6 4.6 %collective-permute-start.2 = (bf16[64,768]{1,0:T(8,128)(2,1)S(1)}, bf16[64,768]{1,0:T(8,128)(2,1)S(1)}, u32[]{:S(2)}, u32[]{:S(2)}) collective-permute-start(bf16[64,768]{1,0:T(8,128)(2,1)S(1)} %get-tuple-element.31), channel_id=1, source_target_pairs={{3,0},{0,1},{1,2},{2,3},{33,32},{34,33},{35,34},{32,35},{7,4},{4,5... | collective-permute-start | bytes 294920 | tf_op jit(solution)/shard_map/ppermute | solution.py:33
  21.7 15.2 %collective-permute-start.8 = (bf16[256,768]{1,0:T(8,128)(2,1)S(1)}, bf16[256,768]{1,0:T(8,128)(2,1)S(1)}, u32[]{:S(2)}, u32[]{:S(2)}) collective-permute-start(bf16[256,768]{1,0:T(8,128)(2,1)S(1)} %pad_maximum_fusion.2.refs_3_), channel_id=1, source_target_pairs={{1,0},{2,1},{3,2},{0,3},{35,32},{32,33},{33,34},{34,35},{5,4},{6,5... | collective-permute-start | bytes 1179656 | tf_op jit(solution)/shard_map/ppermute | solution.py:33
  25.2 11.8 %collective-permute-start.3 = (bf16[256,768]{1,0:T(8,128)(2,1)S(1)}, bf16[256,768]{1,0:T(8,128)(2,1)S(1)}, u32[]{:S(2)}, u32[]{:S(2)}) collective-permute-start(bf16[256,768]{1,0:T(8,128)(2,1)S(1)} %pad_maximum_fusion.1.refs_0_), channel_id=1, source_target_pairs={{8,0},{16,8},{24,16},{0,24},{56,32},{32,40},{40,48},{48,56},{9,1},... | collective-permute-start | bytes 1179656 | tf_op jit(solution)/shard_map/ppermute | solution.py:33
  27.4 18.8 %collective-permute-start.11 = (bf16[264,768]{1,0:T(8,128)(2,1)S(1)}, bf16[264,768]{1,0:T(8,128)(2,1)S(1)}, u32[]{:S(2)}, u32[]{:S(2)}) collective-permute-start(bf16[264,768]{1,0:T(8,128)(2,1)S(1)} %collective-permute-done.10.refs_6_.refs_3_), channel_id=1, source_target_pairs={{32,0},{0,32},{33,1},{1,33},{34,2},{2,34},{35,3},{3,35},{36,4},{4,... | collective-permute-start | bytes 1216520 | tf_op jit(solution)/shard_map/ppermute | solution.py:27
  34.5 9.8 %collective-permute-start.9 = (bf16[256,768]{1,0:T(8,128)(2,1)S(1)}, bf16[256,768]{1,0:T(8,128)(2,1)S(1)}, u32[]{:S(2)}, u32[]{:S(2)}) collective-permute-start(bf16[256,768]{1,0:T(8,128)(2,1)S(1)} %pad_maximum_fusion.2.refs_3_), channel_id=1, source_target_pairs={{3,0},{0,1},{1,2},{2,3},{33,32},{34,33},{35,34},{32,35},{7,4},{4,5... | collective-permute-start | bytes 1179656 | tf_op jit(solution)/shard_map/ppermute | solution.py:33
  37.0 9.2 %collective-permute-start.4 = (bf16[256,768]{1,0:T(8,128)(2,1)S(1)}, bf16[256,768]{1,0:T(8,128)(2,1)S(1)}, u32[]{:S(2)}, u32[]{:S(2)}) collective-permute-start(bf16[256,768]{1,0:T(8,128)(2,1)S(1)} %pad_maximum_fusion.1.refs_0_), channel_id=1, source_target_pairs={{24,0},{0,8},{8,16},{16,24},{40,32},{48,40},{56,48},{32,56},{25,1}... | collective-permute-start | bytes 1179656 | tf_op jit(solution)/shard_map/ppermute | solution.py:33
  37.0 12.7 %collective-permute-start.13 = (bf16[256,768]{1,0:T(8,128)(2,1)S(1)}, bf16[256,768]{1,0:T(8,128)(2,1)S(1)}, u32[]{:S(2)}, u32[]{:S(2)}) collective-permute-start(bf16[256,768]{1,0:T(8,128)(2,1)S(1)} %collective-permute-done.8.refs_4_), channel_id=1, source_target_pairs={{1,0},{2,1},{3,2},{0,3},{35,32},{32,33},{33,34},{34,35},{5,4},{6,5... | collective-permute-start | bytes 1179656 | tf_op jit(solution)/shard_map/ppermute | solution.py:33
  37.0 12.7 %collective-permute-start.12 = (bf16[256,768]{1,0:T(8,128)(2,1)S(1)}, bf16[256,768]{1,0:T(8,128)(2,1)S(1)}, u32[]{:S(2)}, u32[]{:S(2)}) collective-permute-start(bf16[256,768]{1,0:T(8,128)(2,1)S(1)} %collective-permute-done.3.refs_1_), channel_id=1, source_target_pairs={{8,0},{16,8},{24,16},{0,24},{56,32},{32,40},{40,48},{48,56},{9,1},... | collective-permute-start | bytes 1179656 | tf_op jit(solution)/shard_map/ppermute | solution.py:33
  51.0 3.9 %collective-permute-start.14 = (f32[2,8,256]{2,1,0:T(8,128)S(1)}, f32[2,8,256]{2,1,0:T(8,128)S(1)}, u32[]{:S(2)}, u32[]{:S(2)}) collective-permute-start(f32[2,8,256]{2,1,0:T(8,128)S(1)} %get-tuple-element.13.refs_0_.refs_4_), channel_id=1, source_target_pairs={{1,0},{2,1},{3,2},{0,3},{35,32},{32,33},{33,34},{34,35},{5,4},{6,5... | collective-permute-start | bytes 49160 | tf_op jit(solution)/shard_map/ppermute | solution.py:33
  51.1 4.2 %collective-permute-start.15 = (f32[2,8,256]{2,1,0:T(8,128)S(1)}, f32[2,8,256]{2,1,0:T(8,128)S(1)}, u32[]{:S(2)}, u32[]{:S(2)}) collective-permute-start(f32[2,8,256]{2,1,0:T(8,128)S(1)} %get-tuple-element.13.refs_0_.refs_4_), channel_id=1, source_target_pairs={{2,0},{3,1},{0,2},{1,3},{34,32},{35,33},{32,34},{33,35},{6,4},{7,5... | collective-permute-start | bytes 49160 | tf_op jit(solution)/shard_map/ppermute | solution.py:33
  53.8 3.0 %collective-permute-start.16 = (f32[2,8,256]{2,1,0:T(8,128)S(1)}, f32[2,8,256]{2,1,0:T(8,128)S(1)}, u32[]{:S(2)}, u32[]{:S(2)}) collective-permute-start(f32[2,8,256]{2,1,0:T(8,128)S(1)} %get-tuple-element.13.refs_0_.refs_4_), channel_id=1, source_target_pairs={{3,0},{0,1},{1,2},{2,3},{33,32},{34,33},{35,34},{32,35},{7,4},{4,5... | collective-permute-start | bytes 49160 | tf_op jit(solution)/shard_map/ppermute | solution.py:33
  56.9 3.9 %collective-permute-start.17 = (f32[2,8,256]{2,1,0:T(8,128)S(1)}, f32[2,8,256]{2,1,0:T(8,128)S(1)}, u32[]{:S(2)}, u32[]{:S(2)}) collective-permute-start(f32[2,8,256]{2,1,0:T(8,128)S(1)} %shard_map.61.refs_0_), channel_id=1, source_target_pairs={{8,0},{16,8},{24,16},{0,24},{56,32},{32,40},{40,48},{48,56},{9,1},... | collective-permute-start | bytes 49160 | tf_op jit(solution)/shard_map/ppermute | solution.py:33
  58.0 4.1 %collective-permute-start.18 = (f32[2,8,256]{2,1,0:T(8,128)S(1)}, f32[2,8,256]{2,1,0:T(8,128)S(1)}, u32[]{:S(2)}, u32[]{:S(2)}) collective-permute-start(f32[2,8,256]{2,1,0:T(8,128)S(1)} %shard_map.61.refs_0_), channel_id=1, source_target_pairs={{16,0},{24,8},{0,16},{8,24},{48,32},{56,40},{32,48},{40,56},{17,1}... | collective-permute-start | bytes 49160 | tf_op jit(solution)/shard_map/ppermute | solution.py:33
  58.0 4.1 %collective-permute-start.19 = (f32[2,8,256]{2,1,0:T(8,128)S(1)}, f32[2,8,256]{2,1,0:T(8,128)S(1)}, u32[]{:S(2)}, u32[]{:S(2)}) collective-permute-start(f32[2,8,256]{2,1,0:T(8,128)S(1)} %shard_map.61.refs_0_), channel_id=1, source_target_pairs={{24,0},{0,8},{8,16},{16,24},{40,32},{48,40},{56,48},{32,56},{25,1}... | collective-permute-start | bytes 49160 | tf_op jit(solution)/shard_map/ppermute | solution.py:33
  70.9 10.1 %collective-permute-start.20 = (f32[2,4,104,512]{3,2,1,0:T(8,128)S(1)}, f32[2,4,104,512]{3,2,1,0:T(8,128)}, u32[]{:S(2)}, u32[]{:S(2)}) collective-permute-start(f32[2,4,104,512]{3,2,1,0:T(8,128)S(1)} %get-tuple-element.17), channel_id=1, source_target_pairs={{32,0},{0,32},{33,1},{1,33},{34,2},{2,34},{35,3},{3,35},{36,4},{4,... | collective-permute-start | bytes 5111816 | tf_op jit(solution)/shard_map/ppermute | solution.py:27
  83.1 12.3 %collective-permute-start.21 = (f16[104,512]{1,0:T(8,128)(2,1)S(1)}, f16[104,512]{1,0:T(8,128)(2,1)S(1)}, u32[]{:S(2)}, u32[]{:S(2)}) collective-permute-start(f16[104,512]{1,0:T(8,128)(2,1)S(1)} %get-tuple-element.23), channel_id=1, source_target_pairs={{4,0},{68,64},{132,128},{196,192},{0,4},{64,68},{128,132},{192,196... | collective-permute-start | bytes 319496 | tf_op jit(solution)/shard_map/ppermute | solution.py:281
  89.3 8.3 %collective-permute-start.22 = (f16[104,512]{1,0:T(8,128)(2,1)S(1)}, f16[104,512]{1,0:T(8,128)(2,1)S(1)}, u32[]{:S(2)}, u32[]{:S(2)}) collective-permute-start(f16[104,512]{1,0:T(8,128)(2,1)S(1)} %get-tuple-element.29), channel_id=1, source_target_pairs={{192,0},{4,64},{68,128},{132,192},{196,4},{0,68},{64,132},{128,196... | collective-permute-start | bytes 319496 | tf_op jit(solution)/shard_map/ppermute | solution.py:281
  89.8 16.4 %collective-permute-start.23 = (f16[104,512]{1,0:T(8,128)(2,1)S(1)}, f16[104,512]{1,0:T(8,128)(2,1)S(1)}, u32[]{:S(2)}, u32[]{:S(2)}) collective-permute-start(f16[104,512]{1,0:T(8,128)(2,1)S(1)} %get-tuple-element.28), channel_id=1, source_target_pairs={{68,0},{132,64},{196,128},{0,192},{64,4},{128,68},{192,132},{4,196... | collective-permute-start | bytes 319496 | tf_op jit(solution)/shard_map/ppermute | solution.py:281
  92.6 13.7 %collective-permute-start.24 = (f16[104,512]{1,0:T(8,128)(2,1)S(1)}, f16[104,512]{1,0:T(8,128)(2,1)S(1)}, u32[]{:S(2)}, u32[]{:S(2)}) collective-permute-start(f16[104,512]{1,0:T(8,128)(2,1)S(1)} %get-tuple-element.27), channel_id=1, source_target_pairs={{128,0},{192,64},{4,128},{68,192},{132,4},{196,68},{0,132},{64,196... | collective-permute-start | bytes 319496 | tf_op jit(solution)/shard_map/ppermute | solution.py:281
  94.0 12.3 %collective-permute-start.25 = (f16[104,512]{1,0:T(8,128)(2,1)S(1)}, f16[104,512]{1,0:T(8,128)(2,1)S(1)}, u32[]{:S(2)}, u32[]{:S(2)}) collective-permute-start(f16[104,512]{1,0:T(8,128)(2,1)S(1)} %get-tuple-element.26), channel_id=1, source_target_pairs={{132,0},{196,64},{0,128},{64,192},{128,4},{192,68},{4,132},{68,196... | collective-permute-start | bytes 319496 | tf_op jit(solution)/shard_map/ppermute | solution.py:281
  95.4 11.8 %collective-permute-start.26 = (f16[104,512]{1,0:T(8,128)(2,1)S(1)}, f16[104,512]{1,0:T(8,128)(2,1)S(1)}, u32[]{:S(2)}, u32[]{:S(2)}) collective-permute-start(f16[104,512]{1,0:T(8,128)(2,1)S(1)} %get-tuple-element.25), channel_id=1, source_target_pairs={{64,0},{128,64},{192,128},{4,192},{68,4},{132,68},{196,132},{0,196... | collective-permute-start | bytes 319496 | tf_op jit(solution)/shard_map/ppermute | solution.py:281
  97.6 15.1 %copy-start = (s32[512]{0:T(512)S(1)}, s32[512]{0:T(512)}, u32[]{:S(2)}) copy-start(s32[512]{0:T(512)} %param.6) | copy-start | bytes 6148
  97.6 11.2 %collective-permute-start.27 = (f16[104,512]{1,0:T(8,128)(2,1)S(1)}, f16[104,512]{1,0:T(8,128)(2,1)S(1)}, u32[]{:S(2)}, u32[]{:S(2)}) collective-permute-start(f16[104,512]{1,0:T(8,128)(2,1)S(1)} %get-tuple-element.24), channel_id=1, source_target_pairs={{196,0},{0,64},{64,128},{128,192},{192,4},{4,68},{68,132},{132,196... | collective-permute-start | bytes 319496 | tf_op jit(solution)/shard_map/ppermute | solution.py:281
  109.0 11.2 %collective-permute-start.28 = (f16[96,512]{1,0:T(8,128)(2,1)S(1)}, f16[96,512]{1,0:T(8,128)(2,1)S(1)}, u32[]{:S(2)}, u32[]{:S(2)}) collective-permute-start(f16[96,512]{1,0:T(8,128)(2,1)S(1)} %get-tuple-element.19), channel_id=1, source_target_pairs={{64,0},{128,64},{192,128},{0,192},{65,1},{129,65},{193,129},{1,193... | collective-permute-start | bytes 294920 | tf_op jit(solution)/shard_map/ppermute | solution.py:27
  111.9 9.1 %collective-permute-start.29 = (f16[96,512]{1,0:T(8,128)(2,1)S(1)}, f16[96,512]{1,0:T(8,128)(2,1)S(1)}, u32[]{:S(2)}, u32[]{:S(2)}) collective-permute-start(f16[96,512]{1,0:T(8,128)(2,1)S(1)} %get-tuple-element.19), channel_id=1, source_target_pairs={{128,0},{192,64},{0,128},{64,192},{129,1},{193,65},{1,129},{65,193... | collective-permute-start | bytes 294920 | tf_op jit(solution)/shard_map/ppermute | solution.py:27
  111.9 9.1 %collective-permute-start.30 = (f16[96,512]{1,0:T(8,128)(2,1)S(1)}, f16[96,512]{1,0:T(8,128)(2,1)S(1)}, u32[]{:S(2)}, u32[]{:S(2)}) collective-permute-start(f16[96,512]{1,0:T(8,128)(2,1)S(1)} %get-tuple-element.19), channel_id=1, source_target_pairs={{192,0},{0,64},{64,128},{128,192},{193,1},{1,65},{65,129},{129,193... | collective-permute-start | bytes 294920 | tf_op jit(solution)/shard_map/ppermute | solution.py:27
  114.3 19.4 %all-to-all-start = ((f16[32,64,128]{2,1,0:T(8,128)(2,1)}), f16[32,64,128]{2,1,0:T(8,128)(2,1)S(1)}, u32[]{:S(2)}, u32[]{:S(2)}) async-start(f16[32,64,128]{2,1,0:T(8,128)(2,1)} %bitcast.22), calls=%async_computation | async-start | bytes 1048576 | tf_op jit(solution)/shard_map/all_to_all | solution.py:297
  121.3 16.6 %collective-permute-start.31 = (f16[384,512]{1,0:T(8,128)(2,1)S(1)}, f16[384,512]{1,0:T(8,128)(2,1)S(1)}, u32[]{:S(2)}, u32[]{:S(2)}) collective-permute-start(f16[384,512]{1,0:T(8,128)(2,1)S(1)} %bitcast.53), channel_id=1, source_target_pairs={{32,0},{0,32},{33,1},{1,33},{34,2},{2,34},{35,3},{3,35},{36,4},{4,... | collective-permute-start | bytes 1179656 | tf_op jit(solution)/shard_map/ppermute | solution.py:27
  134.9 3.8 %collective-permute-start.32 = (f32[64,128]{1,0:T(8,128)S(1)}, f32[64,128]{1,0:T(8,128)S(1)}, u32[]{:S(2)}, u32[]{:S(2)}) collective-permute-start(f32[64,128]{1,0:T(8,128)S(1)} %get-tuple-element.33), channel_id=1, source_target_pairs={{32,0},{0,32},{33,1},{1,33},{34,2},{2,34},{35,3},{3,35},{36,4},{4,... | collective-permute-start | bytes 98312 | tf_op jit(solution)/shard_map/ppermute | solution.py:27
  138.7 10.3 %collective-permute-start.33 = (f32[2,64,128]{2,1,0:T(8,128)S(1)}, f32[2,64,128]{2,1,0:T(8,128)S(1)}, u32[]{:S(2)}, u32[]{:S(2)}) collective-permute-start(f32[2,64,128]{2,1,0:T(8,128)S(1)} %pad_maximum_fusion.3.refs_0_), channel_id=1, source_target_pairs={{64,0},{128,64},{192,128},{0,192},{65,1},{129,65},{193,129},{1,193... | collective-permute-start | bytes 196616 | tf_op jit(solution)/shard_map/ppermute | solution.py:27
  142.0 9.7 %collective-permute-start.34 = (f32[2,64,128]{2,1,0:T(8,128)S(1)}, f32[2,64,128]{2,1,0:T(8,128)S(1)}, u32[]{:S(2)}, u32[]{:S(2)}) collective-permute-start(f32[2,64,128]{2,1,0:T(8,128)S(1)} %pad_maximum_fusion.3.refs_0_), channel_id=1, source_target_pairs={{128,0},{192,64},{0,128},{64,192},{129,1},{193,65},{1,129},{65,193... | collective-permute-start | bytes 196616 | tf_op jit(solution)/shard_map/ppermute | solution.py:27
  146.7 5.1 %collective-permute-start.35 = (f32[2,64,128]{2,1,0:T(8,128)S(1)}, f32[2,64,128]{2,1,0:T(8,128)S(1)}, u32[]{:S(2)}, u32[]{:S(2)}) collective-permute-start(f32[2,64,128]{2,1,0:T(8,128)S(1)} %pad_maximum_fusion.3.refs_0_), channel_id=1, source_target_pairs={{192,0},{0,64},{64,128},{128,192},{193,1},{1,65},{65,129},{129,193... | collective-permute-start | bytes 196616 | tf_op jit(solution)/shard_map/ppermute | solution.py:27
